TPU v7x, 256 devices: a whole 4x4x8 slice. The times are simulated.
256 devices in a mesh: dp: 32 (over x, z), section: 8 (over y, core).
Axes of the slice: x: 4, y: 4, z: 8, core: 2. Of those that a mesh axis runs over, the one named last changes fastest.
Arguments:
- activations: bfloat16 [8, 64, 512, 4096], P('section', 'dp'), may hold values from -16 to 16
- out_grads: bfloat16 [8, 64, 512, 1024], P('section', 'dp'), may hold values from -16 to 16
- lengths: int32 [64], P('dp'), may hold values from 64 to 512, as said below
Outputs:
- mean_grad: bfloat16 [8, 4096, 1024], P('section', 'dp')
- norm_ratio: float32 [64], P('dp')
Inputs may be any that keep to these rules, and one draw needn't show every extreme that they name: Example e's first lengths[e] token slots are real, the rest padding; some example fills all 512 slots.
All inputs are finite; a program needn't handle non-finite values.
Results may differ from a plain program's by a relative error of at most 0.015.
Values may be sent and summed in bfloat16 or wider, within the bound.
No kernel may reach another device: no remote copies, remote signals or barrier semaphores. Data moves between devices by JAX's collectives and lax.ppermute only.
A program may use at most 128 MiB of HBM per device.

v0:
```python
import math

import jax
import jax.numpy as jnp
from jax import lax
from jax.sharding import Mesh
from jax.sharding import PartitionSpec as P

DP = ("dp_0", "dp_1")


def from_partner(block, axis, distance):
    count = lax.axis_size(axis)
    route = []
    for low in range(count):
        high = low | 1 << distance
        if high != low and high < count:
            route += [(low, high), (high, low)]
    return lax.ppermute(block, axis, route)


def summed_rows(terms, axes):
    running = terms.astype(jnp.bfloat16)
    for axis in axes:
        running = lax.psum_scatter(running, axis, scatter_dimension=0, tiled=True)
    return running.astype(jnp.float32)


def row_term(flat_acts, flat_scaled, layer_index):
    columns = flat_acts[layer_index]
    return lax.dot_general(
        columns,
        flat_scaled[layer_index],
        (((0,), (0,)), ((), ())),
        preferred_element_type=jnp.float32,
    )


def on_device(activations, out_grads, lengths):
    layer_count, example_count, seq_len, model_width = activations.shape
    key_width = out_grads.shape[3]
    total_layers = layer_count * lax.axis_size("section")
    clip_bound = 0.5 * math.sqrt(float(total_layers * seq_len * model_width * key_width))
    positions = lax.broadcasted_iota(jnp.int32, (example_count, seq_len), 1)
    token_keep = (positions < lengths[:, None]).astype(jnp.bfloat16)
    masked = out_grads * token_keep[None, :, :, None]
    act_gram = jnp.einsum(
        "lesd,letd->lest", activations, activations, preferred_element_type=jnp.float32
    )
    grad_gram = jnp.einsum("lesk,letk->lest", masked, masked, preferred_element_type=jnp.float32)
    own_norms = jnp.sum(act_gram * grad_gram, axis=(0, 2, 3))
    levels = lax.axis_size("section").bit_length() - 1
    norm_total = own_norms
    for level_bit in range(levels):
        norm_total = norm_total + from_partner(norm_total, "section", level_bit)
    norm_ratio = jnp.sqrt(norm_total) / clip_bound
    clip_factor = 1.0 / jnp.maximum(norm_ratio, 1.0)
    scaled = (clip_factor[None, :, None, None] * masked).astype(jnp.bfloat16)
    flat_acts = activations.reshape(layer_count, example_count * seq_len, model_width)
    flat_scaled = scaled.reshape(layer_count, example_count * seq_len, key_width)
    examples_all = lax.axis_size(DP) * example_count
    pieces = [summed_rows(row_term(flat_acts, flat_scaled, 0), DP)]
    stacked = jnp.stack(pieces)
    mean_grad = (stacked / examples_all).astype(jnp.bfloat16)
    return (mean_grad, norm_ratio)


def solution(mesh):
    torus = Mesh(mesh.devices.reshape(4, 8, mesh.shape["section"]), ("dp_0", "dp_1", "section"))
    return jax.shard_map(
        on_device,
        mesh=torus,
        in_specs=(P("section", DP, None, None), P("section", DP, None, None), P(DP)),
        out_specs=(P("section", DP, None), P(DP)),
        check_vma=False,
    )
```

profile of v0, /device:TPU:2, one launch (start us, length us, event | category | flops | bytes accessed | tf_op | source)
XLA Modules:
  0.0 189.2 jit_solution(3346332174591074365)
XLA Ops:
  7.2 0.0 reduce-scatter.5.cloned.1.call-start
  7.2 0.7 compare_convert_fusion
  7.9 3.6 %fusion.8 = f32[2,512,512]{2,1,0:T(8,128)S(1)} fusion(bf16[1,2,512,1024]{3,2,1,0:T(8,128)(2,1)} %param.4, bf16[2,512]{1,0:T(2,128)(2,1)S(1)} %compare_convert_fusion), kind=kOutput, calls=%fused_computation.7 | convolution fusion | flops 1074790400 | bytes 4196352 | tf_op jit(solution)/shard_map/lesk,letk->lest/dot_general | solution.py:50
  11.5 0.0 copy-start
  11.5 10.7 %multiply_reduce_fusion = f32[2]{0:T(128)S(1)} fusion(f32[2,512,512]{2,1,0:T(8,128)S(1)} %fusion.8, bf16[1,2,512,4096]{3,2,1,0:T(8,128)(2,1)} %param.3), kind=kOutput, calls=%fused_computation.10 | convolution fusion | flops 4296015872 | bytes 10485768 | tf_op jit(solution)/shard_map/lesd,letd->lest/dot_general | solution.py:47
  22.2 0.0 collective-permute-start
  22.2 1.1 collective-permute-done
  23.4 1.6 collective-permute-start.1
  24.9 2.0 %collective-permute-done.1 = f32[2]{0:T(128)S(1)} collective-permute-done((f32[2]{0:T(128)S(1)}, f32[2]{0:T(128)S(1)}, u32[]{:S(2)}, u32[]{:S(2)}) %collective-permute-start.1) | collective-permute-done | bytes 40 | tf_op jit(solution)/shard_map/ppermute | solution.py:19
  26.9 3.2 %collective-permute-start.2 = (f32[2]{0:T(128)S(1)}, f32[2]{0:T(128)S(1)}, u32[]{:S(2)}, u32[]{:S(2)}) collective-permute-start(f32[2]{0:T(128)S(1)} %add.14), channel_id=1, source_target_pairs={{0,4},{4,0},{1,5},{5,1},{2,6},{6,2},{3,7},{7,3},{8,12},{12,8},{9,1... | collective-permute-start | bytes 32 | tf_op jit(solution)/shard_map/ppermute | solution.py:19
  30.1 1.9 collective-permute-done.2
  32.0 0.5 maximum_divide_fusion
  32.5 0.0 copy-done
  32.5 14.9 %fusion.3 = bf16[4096,1024]{0,1:T(8,128)(2,1)} fusion(bf16[1,2,512,4096]{3,2,1,0:T(8,128)(2,1)} %param.3, f32[2]{0:T(128)S(1)} %get-tuple-element.6, bf16[1,2,512,1024]{3,2,1,0:T(8,128)(2,1)S(1)} %copy-done, bf16[2,512]{1,0:T(2,128)(2,1)S(1)} %compare_convert_fusion), kind=kOutput, calls=%fused_computation.4 | convolution fusion | flops 8598323200 | bytes 18876424 | tf_op jit(solution)/shard_map/dot_general | solution.py:31
  47.4 0.0 reduce-scatter.5.cloned.1.call-update
  47.5 0.0 reduce-scatter.7.cloned.1.call-start
  47.5 84.9 %reduce-scatter.5.cloned.1.call-done = bf16[1024,1024]{0,1:T(8,128)(2,1)} async-done(((bf16[4096,1024]{0,1:T(8,128)(2,1)}), bf16[1024,1024]{0,1:T(8,128)(2,1)}) %reduce-scatter.5.cloned.1.call-update) | async-done | bytes 2097168 | tf_op jit(solution)/shard_map/reduce_scatter | solution.py:25
  132.4 3.9 %copy.10 = bf16[1024,1024]{1,0:T(8,128)(2,1)} copy(bf16[1024,1024]{0,1:T(8,128)(2,1)} %reduce-scatter.5.cloned.1.call-done) | data formatting | bytes 4194304
  136.3 0.0 reduce-scatter.7.cloned.1.call-update
  136.4 43.9 %reduce-scatter.7.cloned.1.call-done = bf16[128,1024]{1,0:T(8,128)(2,1)} async-done(((bf16[1024,1024]{1,0:T(8,128)(2,1)}), bf16[128,1024]{1,0:T(8,128)(2,1)}) %reduce-scatter.7.cloned.1.call-update) | async-done | bytes 262160
  180.3 1.1 copy.11
  181.4 0.1 fusion.17
  181.5 0.9 copy.8
  (2 shorter events, 0.0 us)
Async XLA Ops:
  7.2 125.2 %reduce-scatter.5.cloned.1.call-start = ((), (), s32[]{:S(2)}) async-start(), calls=%async_computation.2 | async-start | bytes 10485760 | tf_op jit(solution)/shard_map/reduce_scatter | solution.py:25
  11.5 21.0 %copy-start = (bf16[1,2,512,1024]{3,2,1,0:T(8,128)(2,1)S(1)}, bf16[1,2,512,1024]{3,2,1,0:T(8,128)(2,1)}, u32[]{:S(2)}) copy-start(bf16[1,2,512,1024]{3,2,1,0:T(8,128)(2,1)} %param.4) | copy-start | bytes 6291460
  22.2 1.2 collective-permute-start
  23.4 3.6 %collective-permute-start.1 = (f32[2]{0:T(128)S(1)}, f32[2]{0:T(128)S(1)}, u32[]{:S(2)}, u32[]{:S(2)}) collective-permute-start(f32[2]{0:T(128)S(1)} %add.13), channel_id=1, source_target_pairs={{0,2},{2,0},{1,3},{3,1},{4,6},{6,4},{5,7},{7,5},{8,10},{10,8},{9,1... | collective-permute-start | bytes 32 | tf_op jit(solution)/shard_map/ppermute | solution.py:19
  26.9 5.1 %collective-permute-start.2 = (f32[2]{0:T(128)S(1)}, f32[2]{0:T(128)S(1)}, u32[]{:S(2)}, u32[]{:S(2)}) collective-permute-start(f32[2]{0:T(128)S(1)} %add.14), channel_id=1, source_target_pairs={{0,4},{4,0},{1,5},{5,1},{2,6},{6,2},{3,7},{7,3},{8,12},{12,8},{9,1... | collective-permute-start | bytes 32 | tf_op jit(solution)/shard_map/ppermute | solution.py:19
  47.5 132.8 %reduce-scatter.7.cloned.1.call-start = ((), (), s32[]{:S(2)}) async-start(), calls=%async_computation.3 | async-start | bytes 2359296
Sparse Core Ops, SparseCore 0:
  47.6 84.7 reduce-scatter.4
  136.5 43.7 reduce-scatter.6
where the time goes:
time: 189 us
  waiting for transfers between devices  134 us (71%)
  matrix products  29.1 us (15%)
  between operations  14.1 us (7%)
  local copies, waits for them, and re-layouts  5.91 us (3%)
  starting transfers between devices  4.87 us (3%)
    reduce_scatter x1, waiting for transfers between devices, summed_rows(): running = lax.psum_scatter(running, axis, scatter_dimension=0, tiled=True)  84.9 us
    unnamed x3, waiting for transfers between devices  44 us
    dot_general x1, matrix products, row_term(): lax.dot_general(columns, flat_scaled[layer_index], (((0,), (0,)), ((), ()...  14.9 us
    dot_general x1, matrix products, on_device(): jnp.einsum('lesd,letd->lest', activations, activations, preferred_element...  10.7 us
    unnamed x5, local copies, waits for them, and re-layouts  5.91 us
    ppermute x3, waiting for transfers between devices, from_partner(): return lax.ppermute(block, axis, route)  5.02 us
    ppermute x3, starting transfers between devices, from_partner(): return lax.ppermute(block, axis, route)  4.79 us
  transfers between devices with their start and end apart: 5, of which 5 were waited for; matrix products, arithmetic and copies ran while one was open for 0% of the time, Pallas kernels for 0%

commit v1 on v0

v1 whole, which is shorter than its diff:
```python
import functools
import math

import jax
import jax.numpy as jnp
from jax import lax
from jax.experimental import pallas as pl
from jax.experimental.pallas import tpu as pltpu
from jax.sharding import Mesh
from jax.sharding import PartitionSpec as P


DP = ("dp_0", "dp_1")
LANES = 128
NORM_STEPS = 4
CHUNK = 256
WHOLE = pl.BlockSpec(memory_space=pltpu.VMEM)


def bf(v):
    return v.astype(jnp.bfloat16)


def f32(v):
    return v.astype(jnp.float32)


def in_hbm(v):
    return pltpu.with_memory_space_constraint(v, pltpu.HBM)


def in_vmem(v):
    return pltpu.with_memory_space_constraint(v, pltpu.VMEM)


def partner_sum(own, level, *order):
    count = lax.axis_size("section")
    moved = lax.ppermute(own, "section", [(i, i ^ 1 << level) for i in range(count)])

    def kernel(own_ref, moved_ref, *refs):
        refs[-1][...] = own_ref[...] + moved_ref[...]

    return call(kernel, [(own.shape, own.dtype)], own, moved, *order)[0]


def chunks(total, body):
    def step(i, _):
        body(pl.ds(pl.multiple_of(i * CHUNK, CHUNK), CHUNK))
        return 0

    lax.fori_loop(0, total // CHUNK, step, 0)


def shift(block, axis, step):
    count = lax.axis_size(axis)
    return lax.ppermute(block, axis, [(i, (i + step) % count) for i in range(count)])


def row_products(left, right):
    return lax.dot_general(left, right, (((1,), (1,)), ((), ())), preferred_element_type=jnp.float32)


def norm_kernel(len_ref, act_ref, grad_ref, norm_ref, top_ref, low_ref):
    j = pl.program_id(0)
    examples, seq, _ = act_ref.shape
    half = seq // 2
    first = j == 0

    def gram(e, _):
        acts = act_ref[e]
        top = row_products(acts[:half], acts)
        low = row_products(acts[half:], acts[half:])
        top_ref[e] = top + jnp.where(first, 0.0, top_ref[e])
        low_ref[e] = low + jnp.where(first, 0.0, low_ref[e])
        return 0

    lax.fori_loop(0, examples, gram, 0)

    def finish(e, _):
        row = lax.broadcasted_iota(jnp.int32, (half, seq), 0)
        col = lax.broadcasted_iota(jnp.int32, (half, seq), 1)
        grads = grad_ref[e]
        size = len_ref[e]
        top = row_products(grads[:half], grads) * top_ref[e]
        low = row_products(grads[half:], grads[half:]) * low_ref[e]
        top = jnp.where((row < size) & (col < size), top, 0.0)
        inner = (row[:, :half] + half < size) & (col[:, :half] + half < size)
        low = jnp.where(inner, low, 0.0)
        total = jnp.sum(top[:, :half]) + 2.0 * jnp.sum(top[:, half:]) + jnp.sum(low)
        norm_ref[e] = jnp.full(norm_ref.shape[1:], total, jnp.float32)
        return 0

    @pl.when(j == pl.num_programs(0) - 1)
    def _():
        lax.fori_loop(0, examples, finish, 0)


def example_norms(acts, grads, lengths):
    examples, seq, width = acts.shape
    key = grads.shape[2]
    tile = width // NORM_STEPS
    half = seq // 2
    return pl.pallas_call(
        norm_kernel,
        grid=(NORM_STEPS,),
        in_specs=[
            pl.BlockSpec(memory_space=pltpu.SMEM),
            pl.BlockSpec((examples, seq, tile), lambda j: (0, 0, j)),
            pl.BlockSpec((examples, seq, key), lambda j: (0, 0, 0)),
        ],
        out_specs=WHOLE,
        out_shape=pltpu.VMEM((examples, 8, LANES), jnp.float32),
        scratch_shapes=[
            pltpu.VMEM((examples, half, seq), jnp.float32),
            pltpu.VMEM((examples, half, half), jnp.float32),
        ],
        compiler_params=pltpu.CompilerParams(
            dimension_semantics=("arbitrary",), vmem_limit_bytes=28 << 20
        ),
        name="example_norms",
    )(lengths, in_hbm(acts), in_hbm(grads))


def on_chip(acts, order):
    def kernel(acts_ref, order_ref, out_ref, tile_ref, sem):
        tile_ref[...] = jnp.zeros_like(tile_ref)
        copy = pltpu.make_async_copy(acts_ref, out_ref, sem)
        copy.start()
        copy.wait()

    return pl.pallas_call(
        kernel,
        in_specs=[pl.BlockSpec(memory_space=pltpu.HBM), WHOLE],
        out_specs=[WHOLE, WHOLE],
        out_shape=[
            pltpu.VMEM(acts.shape, acts.dtype),
            pltpu.VMEM((8, LANES), jnp.float32),
        ],
        scratch_shapes=[pltpu.SemaphoreType.DMA],
        compiler_params=pltpu.CompilerParams(vmem_limit_bytes=2 << 20),
        name="on_chip",
    )(in_hbm(acts), in_vmem(order))


def masked_rows(grads, lengths, order):
    examples, seq, key = grads.shape

    def kernel(len_ref, grad_ref, order_ref, flip_ref, tile_ref):
        tile_ref[...] = jnp.zeros_like(tile_ref)

        def turn(e, _):
            token = lax.broadcasted_iota(jnp.int32, (seq, key), 0)
            masked = jnp.where(token < len_ref[e], f32(grad_ref[e]), 0.0)
            flip_ref[:, pl.ds(pl.multiple_of(e * seq, seq), seq)] = bf(masked).T
            return 0

        lax.fori_loop(0, examples, turn, 0)

    return pl.pallas_call(
        kernel,
        in_specs=[pl.BlockSpec(memory_space=pltpu.SMEM), WHOLE, WHOLE],
        out_specs=[WHOLE, WHOLE],
        out_shape=[
            pltpu.VMEM((key, examples * seq), jnp.bfloat16),
            pltpu.VMEM((8, LANES), jnp.float32),
        ],
        compiler_params=pltpu.CompilerParams(vmem_limit_bytes=16 << 20),
        name="masked_rows",
    )(lengths, grads, in_vmem(order))


def clipped_rows(flipped, total, bound):
    examples = total.shape[0]
    seq = flipped.shape[1] // examples

    def kernel(total_ref, flip_ref, out_ref, ratio_ref):
        clips = []
        for e in range(examples):
            ratio = jnp.sqrt(total_ref[e]) / bound
            ratio_ref[e] = ratio[0, 0]
            clips.append((1.0 / jnp.maximum(ratio, 1.0))[:1, :1])

        def body(rows):
            for e in range(examples):
                part = (rows, slice(e * seq, (e + 1) * seq))
                out_ref[part] = bf(f32(flip_ref[part]) * clips[e])

        chunks(flipped.shape[0], body)

    return pl.pallas_call(
        kernel,
        in_specs=[WHOLE, WHOLE],
        out_specs=[WHOLE, pl.BlockSpec(memory_space=pltpu.SMEM)],
        out_shape=[
            pltpu.VMEM(flipped.shape, flipped.dtype),
            jax.ShapeDtypeStruct((examples,), jnp.float32),
        ],
        compiler_params=pltpu.CompilerParams(vmem_limit_bytes=8 << 20),
        name="clipped_rows",
    )(in_vmem(total), in_vmem(flipped))


def pieces(acts, flipped, ids, outs, step, order):
    examples, seq, _ = acts.shape
    key = flipped.shape[0]

    def kernel(acts_ref, flip_ref, *refs):
        refs = refs[len(order) :]
        refs[-1][...] = jnp.zeros_like(refs[-1])
        blocks = ids()

        def strip(k):
            cols = pl.ds(pl.multiple_of(blocks[k] * LANES, LANES), LANES)
            return acts_ref[:, :, cols].reshape(examples * seq, LANES)

        places = [(out, at) for out, size in zip(refs[:-1], outs) for at in range(size)]

        def rows_of(i, _):
            rows = pl.ds(pl.multiple_of(i * step, step), step)
            for first in range(0, len(places), 4):
                some = range(first, min(first + 4, len(places)))
                block = jnp.concatenate([strip(k) for k in some], 1)
                value = jnp.dot(flip_ref[rows, :], block, preferred_element_type=jnp.float32)
                for q, k in enumerate(some):
                    out, at = places[k]
                    out[at, rows] = bf(value[:, q * LANES : (q + 1) * LANES])
            return 0

        lax.fori_loop(0, key // step, rows_of, 0)

    return pl.pallas_call(
        kernel,
        in_specs=[WHOLE] * (2 + len(order)),
        out_specs=[WHOLE] * (len(outs) + 1),
        out_shape=[pltpu.VMEM((size, key, LANES), jnp.bfloat16) for size in outs]
        + [pltpu.VMEM((8, LANES), jnp.float32)],
        compiler_params=pltpu.CompilerParams(vmem_limit_bytes=12 << 20),
        name="terms",
    )(*[in_vmem(v) for v in (acts, flipped, *order)])


def call(kernel, outs, *args, space=pltpu.VMEM):
    return pl.pallas_call(
        kernel,
        in_specs=[WHOLE] * len(args),
        out_specs=[WHOLE] * len(outs),
        out_shape=[space(shape, dtype) for shape, dtype in outs],
        compiler_params=pltpu.CompilerParams(vmem_limit_bytes=8 << 20),
    )(*[in_vmem(a) for a in args])


def plus(stored, got, skip=0):
    def kernel(stored_ref, got_ref, out_ref, order_ref):
        order_ref[...] = jnp.zeros_like(order_ref)

        def body(rows):
            for k in range(out_ref.shape[0]):
                out_ref[k, rows] = bf(f32(stored_ref[k, rows]) + f32(got_ref[skip + k, rows]))

        chunks(out_ref.shape[1], body)

    outs = [(stored.shape, stored.dtype), ((8, LANES), jnp.float32)]
    return call(kernel, outs, stored, got)


def two_way(acts, flipped, axis, block_id, size):
    count = lax.axis_size(axis)
    far = count // 2
    sent, order = {}, []
    for slot in range(count - 1):
        routes = [(step, slot % 2 if step == 1 else 1 - slot % 2) for step in (1, -1)]
        hops = far - (slot + 1) // 2
        wanted, outs = [(step * hops, half) for step, half in routes], [size, size]
        if slot == count - 2:
            wanted, outs = wanted + [(0, 0), (0, 1)], outs + [2 * size]

        def ids(wanted=wanted):
            index = lax.axis_index(axis)
            return [k for away, half in wanted for k in block_id((index + away) % count, half)]

        *terms, tile = pieces(acts, flipped, ids, outs, 256, order)
        order = [tile]
        for route, term in zip(routes, terms):
            if slot > 1:
                term, tile = plus(term, sent[route])
                order.append(tile)
            sent[route] = shift(term, axis, route[0])
    return terms[2], [[sent[step, half] for step in (1, -1)] for half in (0, 1)]


def x_first(acts, flipped, samples):
    nx, nz = lax.axis_size("dp_0"), lax.axis_size("dp_1")
    key = flipped.shape[0]
    block = ((key, LANES), jnp.bfloat16)

    offsets = {(0, 0): [4, 3], (0, 1): [1, -3], (1, 0): [-1, 2], (1, 1): [-2, 0]}
    steps = (1, -1)

    def terms(*wanted, order):
        def ids():
            x, z = lax.axis_index("dp_0"), lax.axis_index("dp_1")
            return [
                (x + away) % nx * nz + (z + d) % nz
                for parts in wanted
                for batch, half, away in parts
                for d in offsets[batch, half]
            ]

        outs = [2 * len(parts) for parts in wanted]
        return pieces(acts, flipped, ids, outs, 256, order)

    lead = {1: 0, -1: 1}
    far = lambda batch, step: (batch, lead[step], 2 * step)
    lag = lambda batch, step: (batch, 1 - lead[step], step)
    near = lambda batch, step: (batch, lead[step], step)
    own = lambda batch: [(batch, 0, 0), (batch, 1, 0)]

    def send(blocks):
        return {step: shift(block, "dp_0", step) for step, block in zip(steps, blocks)}

    def add(blocks, got, skip):
        outs = [plus(block, got[step], skip) for step, block in zip(steps, blocks)]
        return [out for out, _ in outs], [tile for _, tile in outs]

    def row(refs, k, rows):
        stored, a1, a2, b1, b2 = refs
        one, two = (a1, a2) if k < 2 else (b1, b2)
        return bf(f32(stored[k, rows]) + f32(one[k % 2, rows]) + f32(two[k % 2, rows]))

    def outer_kernel(*refs):
        four, pair, minus_three = refs[5:]

        def body(rows):
            four[rows] = row(refs[:5], 0, rows)
            pair[0, rows] = row(refs[:5], 1, rows)
            pair[1, rows] = row(refs[:5], 2, rows)
            minus_three[rows] = row(refs[:5], 3, rows)

        chunks(key, body)

    def inner_kernel(*refs):
        outs = refs[5:]

        def body(rows):
            for k, out in enumerate(outs):
                out[rows] = row(refs[:5], k, rows)

        chunks(key, body)

    def passed(step, kept, got):
        def kernel(kept_ref, got_ref, out_ref):
            def body(rows):
                came = got_ref[rows] if got_ref.ndim == 2 else got_ref[0, rows]
                out_ref[rows] = bf(f32(kept_ref[rows]) + f32(came))

            chunks(key, body)

        return shift(call(kernel, [block], kept, got)[0], "dp_1", step)

    *blocks, tile = terms(*[[far(0, step)] for step in steps], order=[])
    sent_1 = send(blocks)
    *blocks, tile = terms(*[[lag(0, step), far(1, step)] for step in steps], order=[tile])
    sent_2 = send(blocks)
    *blocks, stored, tile = terms(*[[near(0, step)] for step in steps], own(0), order=[tile])
    blocks, tiles = add(blocks, sent_1, 0)
    sent_3 = send(blocks)
    *blocks, tile = terms(*[[lag(1, step)] for step in steps], order=[tile, *tiles])
    sent_4 = send(blocks)
    *blocks, stored_2, _ = terms(*[[near(1, step)] for step in steps], own(1), order=[tile])
    blocks, _ = add(blocks, sent_2, 2)
    sent_5 = send(blocks)
    outs = [block, ((2, key, LANES), jnp.bfloat16), block]
    came = [sent_3[1], sent_2[-1], sent_2[1], sent_3[-1]]
    four, pair, minus_three = call(outer_kernel, outs, stored, *came)
    pair = shift(pair, "dp_1", 1)
    four = shift(four, "dp_1", -1)
    three = passed(-1, minus_three, four)
    came = [sent_5[1], sent_4[-1], sent_4[1], sent_5[-1]]
    minus_one, two, minus_two, mine = call(inner_kernel, [block] * 4, stored_2, *came)

    ahead = passed(2, two, pair)
    behind = passed(-1, minus_one, passed(-1, minus_two, three))
    return end(samples, mine, ahead, behind, pair)


def end(samples, *terms):
    key = terms[0].shape[0]

    def kernel(*refs):
        def body(rows):
            value = f32(refs[0][rows])
            for ref in refs[1:-1]:
                value = value + f32(ref[rows] if ref.ndim == 2 else ref[1, rows])
            refs[-1][:, rows] = bf(value.T / samples)

        chunks(key, body)

    return call(kernel, [((LANES, key), jnp.bfloat16)], *terms)[0]


def z_first(acts, flipped, samples):
    nx, nz = lax.axis_size("dp_0"), lax.axis_size("dp_1")
    key = flipped.shape[0]
    order = [[2, 1], [-1, 0]]
    block_id = lambda t, half: [(lax.axis_index("dp_0") + d) % nx * nz + t for d in order[half]]
    stored, got = two_way(acts, flipped, "dp_1", block_id, 2)

    def rows_kernel(stored_ref, a1, a2, b1, b2, *outs):
        def body(rows):
            for k, out in enumerate(outs):
                one, two = (a1, a2) if k < 2 else (b1, b2)
                value = f32(stored_ref[k, rows]) + f32(one[k % 2, rows])
                out[rows] = bf(value + f32(two[k % 2, rows]))

        chunks(key, body)

    block = ((key, LANES), jnp.bfloat16)
    *outs, own = call(rows_kernel, [block] * 4, stored, *got[0], *got[1])
    moved = [shift(out, "dp_0", d) for out, d in zip(outs, (2, 1, -1))]
    return end(samples, own, *moved)


def on_device(activations, out_grads, lengths):
    layer_count, example_count, seq_len, model_width = activations.shape
    key_width = out_grads.shape[3]
    total_layers = layer_count * lax.axis_size("section")
    clip_bound = 0.5 * math.sqrt(float(total_layers * seq_len * model_width * key_width))
    acts, grads = activations[0], out_grads[0]
    own = example_norms(acts, grads, lengths)
    pair = partner_sum(own, 0)
    turned, tile = masked_rows(grads, lengths, pair)
    quad = partner_sum(pair, 1, tile)
    stored, tile = on_chip(acts, quad)
    total = partner_sum(quad, 2, tile)
    flipped, norm_ratio = clipped_rows(turned, total, clip_bound)
    samples = float(lax.axis_size(DP) * example_count)
    first = functools.partial(x_first, samples=samples)
    second = functools.partial(z_first, samples=samples)
    mean = lax.cond(lax.axis_index("section") % 2 == 0, first, second, stored, flipped)
    return (mean[None], norm_ratio)


def solution(mesh):
    torus = Mesh(mesh.devices.reshape(4, 8, mesh.shape["section"]), ("dp_0", "dp_1", "section"))
    return jax.shard_map(
        on_device,
        mesh=torus,
        in_specs=(P("section", DP, None, None), P("section", DP, None, None), P(DP)),
        out_specs=(P("section", DP, None), P(DP)),
        check_vma=False,
    )
```

time: 189 us -> 104 us (0.55)
  the two profiles are of different devices: /device:TPU:2 before, /device:TPU:8 now
where the time goes in v1:
time: 104 us
  starting transfers between devices  34.6 us (33%)
  Pallas kernels  33.2 us (32%)
  waiting for transfers between devices  31.8 us (31%)
  local copies, waits for them, and re-layouts  2.69 us (3%)
    ppermute x16, starting transfers between devices, shift(): lax.ppermute(block, axis, [(i, (i + step) % count) for i in range(count)])  31.2 us
    ppermute x16, waiting for transfers between devices, shift(): lax.ppermute(block, axis, [(i, (i + step) % count) for i in range(count)])  30.2 us
    pallas_call x5, Pallas kernels, pieces(): pl.pallas_call(kernel, in_specs=[WHOLE] * (2 + len(order)), out_specs=[WH...  14.7 us
    pallas_call x1, Pallas kernels, example_norms(): pl.pallas_call(norm_kernel, grid=(NORM_STEPS,), in_specs=[pl.BlockSpec(me...  9.47 us
    pallas_call x1, Pallas kernels, on_chip(): pl.pallas_call(kernel, in_specs=[pl.BlockSpec(memory_space=pltpu.HBM), WH...  3.54 us
    ppermute x3, starting transfers between devices, partner_sum(): lax.ppermute(own, 'section', [(i, i ^ 1 << level) for i in range(count)])  3.44 us
    pallas_call x14, Pallas kernels, call(): pl.pallas_call(kernel, in_specs=[WHOLE] * len(args), out_specs=[WHOLE] *...  3.19 us
    unnamed x9, local copies, waits for them, and re-layouts  2.69 us
  transfers between devices with their start and end apart: 19, of which 9 were waited for; matrix products, arithmetic and copies ran while one was open for 0% of the time, Pallas kernels for 19%

profile of v1, /device:TPU:8, one launch (start us, length us, event | category | flops | bytes accessed | tf_op | source)
XLA Modules:
  0.0 103.7 jit_solution(2591476173378642952)
XLA Ops:
  0.6 0.0 copy-start.3
  0.6 0.6 copy-done.3
  1.3 9.5 %example_norms.1.own_ref = f32[2,8,128]{2,1,0:T(8,128)S(1)} custom-call(s32[2]{0:T(128)S(1)} %copy-done.3, bf16[2,512,4096]{2,1,0:T(8,128)(2,1)} %bitcast.8, bf16[2,512,1024]{2,1,0:T(8,128)(2,1)} %bitcast.6), custom_call_target="tpu_custom_call" | custom-call | tf_op jit(solution)/shard_map/example_norms/pallas_call | solution.py:103
  10.8 0.1 collective-permute-start.33
  10.9 1.2 %collective-permute-done.33.moved_ref = f32[2,8,128]{2,1,0:T(8,128)S(1)} collective-permute-done((f32[2,8,128]{2,1,0:T(8,128)S(1)}, f32[2,8,128]{2,1,0:T(8,128)S(1)}, u32[]{:S(2)}, u32[]{:S(2)}) %collective-permute-start.33) | collective-permute-done | bytes 8224 | tf_op jit(solution)/shard_map/ppermute | solution.py:38
  12.0 2.1 %collective-permute-start.34 = (f32[2,8,128]{2,1,0:T(8,128)S(1)}, f32[2,8,128]{2,1,0:T(8,128)S(1)}, u32[]{:S(2)}, u32[]{:S(2)}) collective-permute-start(f32[2,8,128]{2,1,0:T(8,128)S(1)} %shard_map.50.order_ref.own_ref), channel_id=1, source_target_pairs={{0,2},{1,3},{2,0},{3,1},{4,6},{5,7},{6,4},{7,5},{8,10},{9,11},{10,... | collective-permute-start | bytes 24584 | tf_op jit(solution)/shard_map/ppermute | solution.py:38
  14.2 1.2 %masked_rows.1 = (bf16[1024,1024]{1,0:T(8,128)(2,1)S(1)}, f32[8,128]{1,0:T(8,128)S(1)}) custom-call(s32[2]{0:T(128)S(1)} %copy-done.3, bf16[2,512,1024]{2,1,0:T(8,128)(2,1)S(1)} %bitcast.7, f32[2,8,128]{2,1,0:T(8,128)S(1)} %shard_map.50.order_ref.own_ref), custom_call_target="tpu_custom_call" | custom-call | tf_op jit(solution)/shard_map/masked_rows/pallas_call | solution.py:159
  15.4 1.3 %copy-done.1 = bf16[1024,1024]{1,0:T(8,128)(2,1)} copy-done((bf16[1024,1024]{1,0:T(8,128)(2,1)}, bf16[1024,1024]{1,0:T(8,128)(2,1)S(1)}, u32[]{:S(2)}) %copy-start.1) | copy-done | bytes 2097176
  16.8 0.0 collective-permute-done.34.moved_ref
  16.8 1.2 %collective-permute-start.35 = (f32[2,8,128]{2,1,0:T(8,128)S(1)}, f32[2,8,128]{2,1,0:T(8,128)S(1)}, u32[]{:S(2)}, u32[]{:S(2)}) collective-permute-start(f32[2,8,128]{2,1,0:T(8,128)S(1)} %shard_map.51.order_ref.own_ref), channel_id=1, source_target_pairs={{0,4},{1,5},{2,6},{3,7},{4,0},{5,1},{6,2},{7,3},{8,12},{9,13},{10,... | collective-permute-start | bytes 24584 | tf_op jit(solution)/shard_map/ppermute | solution.py:38
  18.0 3.5 %on_chip.1 = (bf16[2,512,4096]{2,1,0:T(8,128)(2,1)S(1)}, f32[8,128]{1,0:T(8,128)S(1)}) custom-call(bf16[2,512,4096]{2,1,0:T(8,128)(2,1)} %bitcast.9, f32[2,8,128]{2,1,0:T(8,128)S(1)} %shard_map.51.order_ref.own_ref), custom_call_target="tpu_custom_call" | custom-call | tf_op jit(solution)/shard_map/on_chip/pallas_call | solution.py:131
  21.5 0.4 collective-permute-done.35.moved_ref
  21.9 0.0 copy-done.2
  21.9 1.0 %clipped_rows.1 = (bf16[1024,1024]{1,0:T(8,128)(2,1)S(1)}, f32[2]{0:T(128)}) custom-call(f32[2,8,128]{2,1,0:T(8,128)S(1)} %shard_map.52.total_ref, bf16[1024,1024]{1,0:T(8,128)(2,1)S(1)} %copy-done.2), custom_call_target="tpu_custom_call" | custom-call | tf_op jit(solution)/shard_map/clipped_rows/pallas_call | solution.py:190
  23.0 80.0 %conditional.1 = (bf16[1,128,1024]{2,1,0:T(8,128)(2,1)S(1)}) conditional(s32[]{:T(128)} %convert_element_type.3, (bf16[2,512,4096]{2,1,0:T(8,128)(2,1)S(1)}, bf16[1024,1024]{1,0:T(8,128)(2,1)S(1)}) %tuple.16, (bf16[2,512,4096]{2,1,0:T(8,128)(2,1)S(1)}, bf16[1024,1024]{1,0:T(8,128)(2,1)S(1)}) %tuple.16), branch_computations={%region_0.1_spmd, %region_1.2_spmd} | conditional | bytes 32506544 | solution.py:439
  23.2 2.1 %terms.19 = (bf16[2,1024,128]{2,1,0:T(8,128)(2,1)S(1)}, bf16[2,1024,128]{2,1,0:T(8,128)(2,1)S(1)}, f32[8,128]{1,0:T(8,128)S(1)}) custom-call(bf16[2,512,4096]{2,1,0:T(8,128)(2,1)S(1)} %get-tuple-element.57.acts_ref, bf16[1024,1024]{1,0:T(8,128)(2,1)S(1)} %get-tuple-element.58.flip_ref), custom_call_target="tpu_custom_call" | custom-call | tf_op jit(solution)/shard_map/cond/branch_1_fun/terms/pallas_call | solution.py:231
  25.4 2.8 %collective-permute-start.18 = (bf16[2,1024,128]{2,1,0:T(8,128)(2,1)S(1)}, bf16[2,1024,128]{2,1,0:T(8,128)(2,1)S(1)}, u32[]{:S(2)}, u32[]{:S(2)}) collective-permute-start(bf16[2,1024,128]{2,1,0:T(8,128)(2,1)S(1)} %get-tuple-element.66), channel_id=1, source_target_pairs={{0,192},{64,0},{128,64},{192,128},{1,193},{65,1},{129,65},{193,129... | collective-permute-start | bytes 1572872 | tf_op jit(solution)/shard_map/cond/branch_1_fun/ppermute | solution.py:56
  28.2 3.4 %terms.20 = (bf16[4,1024,128]{2,1,0:T(8,128)(2,1)S(1)}, bf16[4,1024,128]{2,1,0:T(8,128)(2,1)S(1)}, f32[8,128]{1,0:T(8,128)S(1)}) custom-call(bf16[2,512,4096]{2,1,0:T(8,128)(2,1)S(1)} %get-tuple-element.57.acts_ref, bf16[1024,1024]{1,0:T(8,128)(2,1)S(1)} %get-tuple-element.58.flip_ref, f32[8,128]{1,0:T(8,128)S(1)} %get-tuple-element.59.refs_0_), custom_call_target="tpu_custom_call" | custom-call | tf_op jit(solution)/shard_map/cond/branch_1_fun/terms/pallas_call | solution.py:231
  31.6 0.1 collective-permute-start.19
  31.7 0.8 collective-permute-start.17
  32.4 2.6 %collective-permute-start.23 = (bf16[4,1024,128]{2,1,0:T(8,128)(2,1)S(1)}, bf16[4,1024,128]{2,1,0:T(8,128)(2,1)S(1)}, u32[]{:S(2)}, u32[]{:S(2)}) collective-permute-start(bf16[4,1024,128]{2,1,0:T(8,128)(2,1)S(1)} %get-tuple-element.76), channel_id=1, source_target_pairs={{0,192},{64,0},{128,64},{192,128},{1,193},{65,1},{129,65},{193,129... | collective-permute-start | bytes 3145736 | tf_op jit(solution)/shard_map/cond/branch_1_fun/ppermute | solution.py:56
  35.0 3.4 %terms.21 = (bf16[2,1024,128]{2,1,0:T(8,128)(2,1)S(1)}, bf16[2,1024,128]{2,1,0:T(8,128)(2,1)S(1)}, bf16[4,1024,128]{2,1,0:T(8,128)(2,1)S(1)}, f32[8,128]{1,0:T(8,128)S(1)}) custom-call(bf16[2,512,4096]{2,1,0:T(8,128)(2,1)S(1)} %get-tuple-element.57.acts_ref, bf16[1024,1024]{1,0:T(8,128)(2,1)S(1)} %get-tuple-element.58.flip_ref, ...), custom_call_target="tpu_custom_call" | custom-call | tf_op jit(solution)/shard_map/cond/branch_1_fun/terms/pallas_call | solution.py:231
  38.4 0.0 collective-permute-done.18.got_ref
  38.4 0.1 branch_1_fun.12
  38.5 2.0 %collective-permute-start.26 = (bf16[2,1024,128]{2,1,0:T(8,128)(2,1)S(1)}, bf16[2,1024,128]{2,1,0:T(8,128)(2,1)S(1)}, u32[]{:S(2)}, u32[]{:S(2)}) collective-permute-start(bf16[2,1024,128]{2,1,0:T(8,128)(2,1)S(1)} %get-tuple-element.82), channel_id=1, source_target_pairs={{0,192},{64,0},{128,64},{192,128},{1,193},{65,1},{129,65},{193,129... | collective-permute-start | bytes 1572872 | tf_op jit(solution)/shard_map/cond/branch_1_fun/ppermute | solution.py:56
  40.5 12.7 %collective-permute-done.17.got_ref = bf16[2,1024,128]{2,1,0:T(8,128)(2,1)S(1)} collective-permute-done((bf16[2,1024,128]{2,1,0:T(8,128)(2,1)S(1)}, bf16[2,1024,128]{2,1,0:T(8,128)(2,1)S(1)}, u32[]{:S(2)}, u32[]{:S(2)}) %collective-permute-start.17) | collective-permute-done | bytes 524320 | tf_op jit(solution)/shard_map/cond/branch_1_fun/ppermute | solution.py:56
  53.3 0.1 branch_1_fun.11
  53.4 0.1 collective-permute-start.25
  53.5 2.1 %terms.22 = (bf16[2,1024,128]{2,1,0:T(8,128)(2,1)S(1)}, bf16[2,1024,128]{2,1,0:T(8,128)(2,1)S(1)}, f32[8,128]{1,0:T(8,128)S(1)}) custom-call(bf16[2,512,4096]{2,1,0:T(8,128)(2,1)S(1)} %get-tuple-element.57.acts_ref, bf16[1024,1024]{1,0:T(8,128)(2,1)S(1)} %get-tuple-element.58.flip_ref, f32[8,128]{1,0:T(8,128)S(1)} %get-tuple-element.61.refs_0_, ...), custom_call_target="tpu_custom_call" | custom-call | tf_op jit(solution)/shard_map/cond/branch_1_fun/terms/pallas_call | solution.py:231
  55.7 3.3 %collective-permute-start.21 = (bf16[2,1024,128]{2,1,0:T(8,128)(2,1)S(1)}, bf16[2,1024,128]{2,1,0:T(8,128)(2,1)S(1)}, u32[]{:S(2)}, u32[]{:S(2)}) collective-permute-start(bf16[2,1024,128]{2,1,0:T(8,128)(2,1)S(1)} %get-tuple-element.73), channel_id=1, source_target_pairs={{0,192},{64,0},{128,64},{192,128},{1,193},{65,1},{129,65},{193,129... | collective-permute-start | bytes 1572872 | tf_op jit(solution)/shard_map/cond/branch_1_fun/ppermute | solution.py:56
  58.9 3.7 %terms.23 = (bf16[2,1024,128]{2,1,0:T(8,128)(2,1)S(1)}, bf16[2,1024,128]{2,1,0:T(8,128)(2,1)S(1)}, bf16[4,1024,128]{2,1,0:T(8,128)(2,1)S(1)}, f32[8,128]{1,0:T(8,128)}) custom-call(bf16[2,512,4096]{2,1,0:T(8,128)(2,1)S(1)} %get-tuple-element.57.acts_ref, bf16[1024,1024]{1,0:T(8,128)(2,1)S(1)} %get-tuple-element.58.flip_ref, ...), custom_call_target="tpu_custom_call" | custom-call | tf_op jit(solution)/shard_map/cond/branch_1_fun/terms/pallas_call | solution.py:231
  62.7 0.0 collective-permute-done.19.got_ref.refs_3_
  62.7 0.0 collective-permute-start.22
  62.7 0.0 collective-permute-done.23.got_ref.refs_2_
  62.7 0.0 collective-permute-done.26.refs_4_
  62.7 1.2 %collective-permute-done.25.refs_1_ = bf16[2,1024,128]{2,1,0:T(8,128)(2,1)S(1)} collective-permute-done((bf16[2,1024,128]{2,1,0:T(8,128)(2,1)S(1)}, bf16[2,1024,128]{2,1,0:T(8,128)(2,1)S(1)}, u32[]{:S(2)}, u32[]{:S(2)}) %collective-permute-start.25) | collective-permute-done | bytes 524320 | tf_op jit(solution)/shard_map/cond/branch_1_fun/ppermute | solution.py:56
  63.9 0.4 branch_1_fun.16
  64.3 5.9 %collective-permute-start.29 = (bf16[1024,128]{1,0:T(8,128)(2,1)S(1)}, bf16[1024,128]{1,0:T(8,128)(2,1)S(1)}, u32[]{:S(2)}, u32[]{:S(2)}) collective-permute-start(bf16[1024,128]{1,0:T(8,128)(2,1)S(1)} %get-tuple-element.87), channel_id=1, source_target_pairs={{0,56},{8,0},{16,8},{24,16},{32,24},{40,32},{48,40},{56,48},{1,57}... | collective-permute-start | bytes 786440 | tf_op jit(solution)/shard_map/cond/branch_1_fun/ppermute | solution.py:56
  70.2 0.7 branch_1_fun.13
  70.9 0.0 collective-permute-start.20
  70.9 0.7 branch_1_fun.14
  71.6 3.2 %collective-permute-start.24 = (bf16[2,1024,128]{2,1,0:T(8,128)(2,1)S(1)}, bf16[2,1024,128]{2,1,0:T(8,128)(2,1)S(1)}, u32[]{:S(2)}, u32[]{:S(2)}) collective-permute-start(bf16[2,1024,128]{2,1,0:T(8,128)(2,1)S(1)} %get-tuple-element.77), channel_id=1, source_target_pairs={{0,192},{64,0},{128,64},{192,128},{1,193},{65,1},{129,65},{193,129... | collective-permute-start | bytes 1572872 | tf_op jit(solution)/shard_map/cond/branch_1_fun/ppermute | solution.py:56
  74.8 0.0 collective-permute-done.29.got_ref
  74.8 0.0 collective-permute-start.27
  74.8 0.1 branch_1_fun.18
  74.9 0.0 collective-permute-done.21.refs_2_
  74.9 3.3 %collective-permute-start.30 = (bf16[1024,128]{1,0:T(8,128)(2,1)S(1)}, bf16[1024,128]{1,0:T(8,128)(2,1)S(1)}, u32[]{:S(2)}, u32[]{:S(2)}) collective-permute-start(bf16[1024,128]{1,0:T(8,128)(2,1)S(1)} %branch_1_fun.18), channel_id=1, source_target_pairs={{0,56},{8,0},{16,8},{24,16},{32,24},{40,32},{48,40},{56,48},{1,57}... | collective-permute-start | bytes 786440 | tf_op jit(solution)/shard_map/cond/branch_1_fun/ppermute | solution.py:56
  78.2 0.0 collective-permute-done.22.refs_3_
  78.2 7.3 %collective-permute-done.20.refs_1_ = bf16[2,1024,128]{2,1,0:T(8,128)(2,1)S(1)} collective-permute-done((bf16[2,1024,128]{2,1,0:T(8,128)(2,1)S(1)}, bf16[2,1024,128]{2,1,0:T(8,128)(2,1)S(1)}, u32[]{:S(2)}, u32[]{:S(2)}) %collective-permute-start.20) | collective-permute-done | bytes 524320 | tf_op jit(solution)/shard_map/cond/branch_1_fun/ppermute | solution.py:56
  85.5 1.3 %collective-permute-done.24.refs_4_ = bf16[2,1024,128]{2,1,0:T(8,128)(2,1)S(1)} collective-permute-done((bf16[2,1024,128]{2,1,0:T(8,128)(2,1)S(1)}, bf16[2,1024,128]{2,1,0:T(8,128)(2,1)S(1)}, u32[]{:S(2)}, u32[]{:S(2)}) %collective-permute-start.24) | collective-permute-done | bytes 524320 | tf_op jit(solution)/shard_map/cond/branch_1_fun/ppermute | solution.py:56
  86.9 0.4 branch_1_fun.15
  87.3 0.0 collective-permute-done.30.got_ref
  87.3 0.1 branch_1_fun.19
  87.4 3.3 %collective-permute-start.31 = (bf16[1024,128]{1,0:T(8,128)(2,1)S(1)}, bf16[1024,128]{1,0:T(8,128)(2,1)S(1)}, u32[]{:S(2)}, u32[]{:S(2)}) collective-permute-start(bf16[1024,128]{1,0:T(8,128)(2,1)S(1)} %branch_1_fun.19), channel_id=1, source_target_pairs={{0,56},{8,0},{16,8},{24,16},{32,24},{40,32},{48,40},{56,48},{1,57}... | collective-permute-start | bytes 786440 | tf_op jit(solution)/shard_map/cond/branch_1_fun/ppermute | solution.py:56
  90.7 0.0 collective-permute-done.27.got_ref.refs_3_
  90.7 0.1 branch_1_fun.17
  90.8 0.1 collective-permute-start.28
  90.8 3.7 %collective-permute-done.31.got_ref = bf16[1024,128]{1,0:T(8,128)(2,1)S(1)} collective-permute-done((bf16[1024,128]{1,0:T(8,128)(2,1)S(1)}, bf16[1024,128]{1,0:T(8,128)(2,1)S(1)}, u32[]{:S(2)}, u32[]{:S(2)}) %collective-permute-start.31) | collective-permute-done | bytes 262176 | tf_op jit(solution)/shard_map/cond/branch_1_fun/ppermute | solution.py:56
  94.6 0.1 branch_1_fun.20
  94.6 3.8 %collective-permute-start.32 = (bf16[1024,128]{1,0:T(8,128)(2,1)S(1)}, bf16[1024,128]{1,0:T(8,128)(2,1)S(1)}, u32[]{:S(2)}, u32[]{:S(2)}) collective-permute-start(bf16[1024,128]{1,0:T(8,128)(2,1)S(1)} %branch_1_fun.20), channel_id=1, source_target_pairs={{0,56},{8,0},{16,8},{24,16},{32,24},{40,32},{48,40},{56,48},{1,57}... | collective-permute-start | bytes 786440 | tf_op jit(solution)/shard_map/cond/branch_1_fun/ppermute | solution.py:56
  98.4 3.1 %collective-permute-done.28.refs_1_ = bf16[1024,128]{1,0:T(8,128)(2,1)S(1)} collective-permute-done((bf16[1024,128]{1,0:T(8,128)(2,1)S(1)}, bf16[1024,128]{1,0:T(8,128)(2,1)S(1)}, u32[]{:S(2)}, u32[]{:S(2)}) %collective-permute-start.28) | collective-permute-done | bytes 262176 | tf_op jit(solution)/shard_map/cond/branch_1_fun/ppermute | solution.py:56
  101.6 0.7 collective-permute-done.32.refs_2_
  102.3 0.4 branch_1_fun.21
  103.0 0.7 copy.7
  (7 shorter events, 0.0 us)
Async XLA Ops:
  0.6 0.7 copy-start.3
  1.3 12.9 %copy-start = (bf16[1,2,512,1024]{3,2,1,0:T(8,128)(2,1)S(1)}, bf16[1,2,512,1024]{3,2,1,0:T(8,128)(2,1)}, u32[]{:S(2)}) copy-start(bf16[1,2,512,1024]{3,2,1,0:T(8,128)(2,1)} %param.6) | copy-start | bytes 6291460
  10.8 1.3 %collective-permute-start.33 = (f32[2,8,128]{2,1,0:T(8,128)S(1)}, f32[2,8,128]{2,1,0:T(8,128)S(1)}, u32[]{:S(2)}, u32[]{:S(2)}) collective-permute-start(f32[2,8,128]{2,1,0:T(8,128)S(1)} %example_norms.1.own_ref), channel_id=1, source_target_pairs={{0,1},{1,0},{2,3},{3,2},{4,5},{5,4},{6,7},{7,6},{8,9},{9,8},{10,11... | collective-permute-start | bytes 24584 | tf_op jit(solution)/shard_map/ppermute | solution.py:38
  12.0 4.7 %collective-permute-start.34 = (f32[2,8,128]{2,1,0:T(8,128)S(1)}, f32[2,8,128]{2,1,0:T(8,128)S(1)}, u32[]{:S(2)}, u32[]{:S(2)}) collective-permute-start(f32[2,8,128]{2,1,0:T(8,128)S(1)} %shard_map.50.order_ref.own_ref), channel_id=1, source_target_pairs={{0,2},{1,3},{2,0},{3,1},{4,6},{5,7},{6,4},{7,5},{8,10},{9,11},{10,... | collective-permute-start | bytes 24584 | tf_op jit(solution)/shard_map/ppermute | solution.py:38
  15.4 1.3 %copy-start.1 = (bf16[1024,1024]{1,0:T(8,128)(2,1)}, bf16[1024,1024]{1,0:T(8,128)(2,1)S(1)}, u32[]{:S(2)}) copy-start(bf16[1024,1024]{1,0:T(8,128)(2,1)S(1)} %get-tuple-element.99.flip_ref) | copy-start | bytes 6291460
  16.8 5.2 %collective-permute-start.35 = (f32[2,8,128]{2,1,0:T(8,128)S(1)}, f32[2,8,128]{2,1,0:T(8,128)S(1)}, u32[]{:S(2)}, u32[]{:S(2)}) collective-permute-start(f32[2,8,128]{2,1,0:T(8,128)S(1)} %shard_map.51.order_ref.own_ref), channel_id=1, source_target_pairs={{0,4},{1,5},{2,6},{3,7},{4,0},{5,1},{6,2},{7,3},{8,12},{9,13},{10,... | collective-permute-start | bytes 24584 | tf_op jit(solution)/shard_map/ppermute | solution.py:38
  18.0 4.0 %copy-start.2 = (bf16[1024,1024]{1,0:T(8,128)(2,1)S(1)}, bf16[1024,1024]{1,0:T(8,128)(2,1)}, u32[]{:S(2)}) copy-start(bf16[1024,1024]{1,0:T(8,128)(2,1)} %copy-done.1) | copy-start | bytes 6291460
  25.4 13.0 %collective-permute-start.18 = (bf16[2,1024,128]{2,1,0:T(8,128)(2,1)S(1)}, bf16[2,1024,128]{2,1,0:T(8,128)(2,1)S(1)}, u32[]{:S(2)}, u32[]{:S(2)}) collective-permute-start(bf16[2,1024,128]{2,1,0:T(8,128)(2,1)S(1)} %get-tuple-element.66), channel_id=1, source_target_pairs={{0,192},{64,0},{128,64},{192,128},{1,193},{65,1},{129,65},{193,129... | collective-permute-start | bytes 1572872 | tf_op jit(solution)/shard_map/cond/branch_1_fun/ppermute | solution.py:56
  31.6 31.1 %collective-permute-start.19 = (bf16[4,1024,128]{2,1,0:T(8,128)(2,1)S(1)}, bf16[4,1024,128]{2,1,0:T(8,128)(2,1)S(1)}, u32[]{:S(2)}, u32[]{:S(2)}) collective-permute-start(bf16[4,1024,128]{2,1,0:T(8,128)(2,1)S(1)} %get-tuple-element.71), channel_id=1, source_target_pairs={{0,64},{64,128},{128,192},{192,0},{1,65},{65,129},{129,193},{193,1... | collective-permute-start | bytes 3145736 | tf_op jit(solution)/shard_map/cond/branch_1_fun/ppermute | solution.py:56
  31.7 21.6 %collective-permute-start.17 = (bf16[2,1024,128]{2,1,0:T(8,128)(2,1)S(1)}, bf16[2,1024,128]{2,1,0:T(8,128)(2,1)S(1)}, u32[]{:S(2)}, u32[]{:S(2)}) collective-permute-start(bf16[2,1024,128]{2,1,0:T(8,128)(2,1)S(1)} %get-tuple-element.63), channel_id=1, source_target_pairs={{0,64},{64,128},{128,192},{192,0},{1,65},{65,129},{129,193},{193,1... | collective-permute-start | bytes 1572872 | tf_op jit(solution)/shard_map/cond/branch_1_fun/ppermute | solution.py:56
  32.4 30.2 %collective-permute-start.23 = (bf16[4,1024,128]{2,1,0:T(8,128)(2,1)S(1)}, bf16[4,1024,128]{2,1,0:T(8,128)(2,1)S(1)}, u32[]{:S(2)}, u32[]{:S(2)}) collective-permute-start(bf16[4,1024,128]{2,1,0:T(8,128)(2,1)S(1)} %get-tuple-element.76), channel_id=1, source_target_pairs={{0,192},{64,0},{128,64},{192,128},{1,193},{65,1},{129,65},{193,129... | collective-permute-start | bytes 3145736 | tf_op jit(solution)/shard_map/cond/branch_1_fun/ppermute | solution.py:56
  38.5 24.2 %collective-permute-start.26 = (bf16[2,1024,128]{2,1,0:T(8,128)(2,1)S(1)}, bf16[2,1024,128]{2,1,0:T(8,128)(2,1)S(1)}, u32[]{:S(2)}, u32[]{:S(2)}) collective-permute-start(bf16[2,1024,128]{2,1,0:T(8,128)(2,1)S(1)} %get-tuple-element.82), channel_id=1, source_target_pairs={{0,192},{64,0},{128,64},{192,128},{1,193},{65,1},{129,65},{193,129... | collective-permute-start | bytes 1572872 | tf_op jit(solution)/shard_map/cond/branch_1_fun/ppermute | solution.py:56
  53.4 10.5 %collective-permute-start.25 = (bf16[2,1024,128]{2,1,0:T(8,128)(2,1)S(1)}, bf16[2,1024,128]{2,1,0:T(8,128)(2,1)S(1)}, u32[]{:S(2)}, u32[]{:S(2)}) collective-permute-start(bf16[2,1024,128]{2,1,0:T(8,128)(2,1)S(1)} %get-tuple-element.81), channel_id=1, source_target_pairs={{0,64},{64,128},{128,192},{192,0},{1,65},{65,129},{129,193},{193,1... | collective-permute-start | bytes 1572872 | tf_op jit(solution)/shard_map/cond/branch_1_fun/ppermute | solution.py:56
  55.7 19.3 %collective-permute-start.21 = (bf16[2,1024,128]{2,1,0:T(8,128)(2,1)S(1)}, bf16[2,1024,128]{2,1,0:T(8,128)(2,1)S(1)}, u32[]{:S(2)}, u32[]{:S(2)}) collective-permute-start(bf16[2,1024,128]{2,1,0:T(8,128)(2,1)S(1)} %get-tuple-element.73), channel_id=1, source_target_pairs={{0,192},{64,0},{128,64},{192,128},{1,193},{65,1},{129,65},{193,129... | collective-permute-start | bytes 1572872 | tf_op jit(solution)/shard_map/cond/branch_1_fun/ppermute | solution.py:56
  62.7 15.6 %collective-permute-start.22 = (bf16[2,1024,128]{2,1,0:T(8,128)(2,1)S(1)}, bf16[2,1024,128]{2,1,0:T(8,128)(2,1)S(1)}, u32[]{:S(2)}, u32[]{:S(2)}) collective-permute-start(bf16[2,1024,128]{2,1,0:T(8,128)(2,1)S(1)} %get-tuple-element.74), channel_id=1, source_target_pairs={{0,64},{64,128},{128,192},{192,0},{1,65},{65,129},{129,193},{193,1... | collective-permute-start | bytes 1572872 | tf_op jit(solution)/shard_map/cond/branch_1_fun/ppermute | solution.py:56
  64.3 10.5 %collective-permute-start.29 = (bf16[1024,128]{1,0:T(8,128)(2,1)S(1)}, bf16[1024,128]{1,0:T(8,128)(2,1)S(1)}, u32[]{:S(2)}, u32[]{:S(2)}) collective-permute-start(bf16[1024,128]{1,0:T(8,128)(2,1)S(1)} %get-tuple-element.87), channel_id=1, source_target_pairs={{0,56},{8,0},{16,8},{24,16},{32,24},{40,32},{48,40},{56,48},{1,57}... | collective-permute-start | bytes 786440 | tf_op jit(solution)/shard_map/cond/branch_1_fun/ppermute | solution.py:56
  70.9 14.7 %collective-permute-start.20 = (bf16[2,1024,128]{2,1,0:T(8,128)(2,1)S(1)}, bf16[2,1024,128]{2,1,0:T(8,128)(2,1)S(1)}, u32[]{:S(2)}, u32[]{:S(2)}) collective-permute-start(bf16[2,1024,128]{2,1,0:T(8,128)(2,1)S(1)} %get-tuple-element.72), channel_id=1, source_target_pairs={{0,64},{64,128},{128,192},{192,0},{1,65},{65,129},{129,193},{193,1... | collective-permute-start | bytes 1572872 | tf_op jit(solution)/shard_map/cond/branch_1_fun/ppermute | solution.py:56
  71.6 15.3 %collective-permute-start.24 = (bf16[2,1024,128]{2,1,0:T(8,128)(2,1)S(1)}, bf16[2,1024,128]{2,1,0:T(8,128)(2,1)S(1)}, u32[]{:S(2)}, u32[]{:S(2)}) collective-permute-start(bf16[2,1024,128]{2,1,0:T(8,128)(2,1)S(1)} %get-tuple-element.77), channel_id=1, source_target_pairs={{0,192},{64,0},{128,64},{192,128},{1,193},{65,1},{129,65},{193,129... | collective-permute-start | bytes 1572872 | tf_op jit(solution)/shard_map/cond/branch_1_fun/ppermute | solution.py:56
  74.8 15.9 %collective-permute-start.27 = (bf16[2,1024,128]{2,1,0:T(8,128)(2,1)S(1)}, bf16[2,1024,128]{2,1,0:T(8,128)(2,1)S(1)}, u32[]{:S(2)}, u32[]{:S(2)}) collective-permute-start(bf16[2,1024,128]{2,1,0:T(8,128)(2,1)S(1)} %get-tuple-element.83), channel_id=1, source_target_pairs={{0,8},{8,16},{16,24},{24,32},{32,40},{40,48},{48,56},{56,0},{1,9},... | collective-permute-start | bytes 1572872 | tf_op jit(solution)/shard_map/cond/branch_1_fun/ppermute | solution.py:56
  74.9 12.3 %collective-permute-start.30 = (bf16[1024,128]{1,0:T(8,128)(2,1)S(1)}, bf16[1024,128]{1,0:T(8,128)(2,1)S(1)}, u32[]{:S(2)}, u32[]{:S(2)}) collective-permute-start(bf16[1024,128]{1,0:T(8,128)(2,1)S(1)} %branch_1_fun.18), channel_id=1, source_target_pairs={{0,56},{8,0},{16,8},{24,16},{32,24},{40,32},{48,40},{56,48},{1,57}... | collective-permute-start | bytes 786440 | tf_op jit(solution)/shard_map/cond/branch_1_fun/ppermute | solution.py:56
  87.4 7.2 %collective-permute-start.31 = (bf16[1024,128]{1,0:T(8,128)(2,1)S(1)}, bf16[1024,128]{1,0:T(8,128)(2,1)S(1)}, u32[]{:S(2)}, u32[]{:S(2)}) collective-permute-start(bf16[1024,128]{1,0:T(8,128)(2,1)S(1)} %branch_1_fun.19), channel_id=1, source_target_pairs={{0,56},{8,0},{16,8},{24,16},{32,24},{40,32},{48,40},{56,48},{1,57}... | collective-permute-start | bytes 786440 | tf_op jit(solution)/shard_map/cond/branch_1_fun/ppermute | solution.py:56
  90.8 10.8 %collective-permute-start.28 = (bf16[1024,128]{1,0:T(8,128)(2,1)S(1)}, bf16[1024,128]{1,0:T(8,128)(2,1)S(1)}, u32[]{:S(2)}, u32[]{:S(2)}) collective-permute-start(bf16[1024,128]{1,0:T(8,128)(2,1)S(1)} %branch_1_fun.17), channel_id=1, source_target_pairs={{0,16},{8,24},{16,32},{24,40},{32,48},{40,56},{48,0},{56,8},{1,17}... | collective-permute-start | bytes 786440 | tf_op jit(solution)/shard_map/cond/branch_1_fun/ppermute | solution.py:56
  94.6 7.7 %collective-permute-start.32 = (bf16[1024,128]{1,0:T(8,128)(2,1)S(1)}, bf16[1024,128]{1,0:T(8,128)(2,1)S(1)}, u32[]{:S(2)}, u32[]{:S(2)}) collective-permute-start(bf16[1024,128]{1,0:T(8,128)(2,1)S(1)} %branch_1_fun.20), channel_id=1, source_target_pairs={{0,56},{8,0},{16,8},{24,16},{32,24},{40,32},{48,40},{56,48},{1,57}... | collective-permute-start | bytes 786440 | tf_op jit(solution)/shard_map/cond/branch_1_fun/ppermute | solution.py:56

commit v2 on v1

--- a/solution.py
+++ b/solution.py
@@ -12,7 +12,7 @@
 
 DP = ("dp_0", "dp_1")
 LANES = 128
-NORM_STEPS = 4
+NORM_STEPS = 2
 CHUNK = 256
 WHOLE = pl.BlockSpec(memory_space=pltpu.VMEM)
 
@@ -60,11 +60,16 @@
     return lax.dot_general(left, right, (((1,), (1,)), ((), ())), preferred_element_type=jnp.float32)
 
 
-def norm_kernel(len_ref, act_ref, grad_ref, norm_ref, top_ref, low_ref):
+def norm_kernel(len_src, act_ref, grad_ref, norm_ref, top_ref, low_ref, len_ref, sem):
     j = pl.program_id(0)
     examples, seq, _ = act_ref.shape
     half = seq // 2
     first = j == 0
+    load = pltpu.make_async_copy(len_src, len_ref, sem)
+
+    @pl.when(first)
+    def _():
+        load.start()
 
     def gram(e, _):
         acts = act_ref[e]
@@ -75,6 +80,10 @@
         return 0
 
     lax.fori_loop(0, examples, gram, 0)
+
+    @pl.when(first)
+    def _():
+        load.wait()
 
     def finish(e, _):
         row = lax.broadcasted_iota(jnp.int32, (half, seq), 0)
@@ -104,7 +113,7 @@
         norm_kernel,
         grid=(NORM_STEPS,),
         in_specs=[
-            pl.BlockSpec(memory_space=pltpu.SMEM),
+            pl.BlockSpec(memory_space=pltpu.HBM),
             pl.BlockSpec((examples, seq, tile), lambda j: (0, 0, j)),
             pl.BlockSpec((examples, seq, key), lambda j: (0, 0, 0)),
         ],
@@ -113,12 +122,14 @@
         scratch_shapes=[
             pltpu.VMEM((examples, half, seq), jnp.float32),
             pltpu.VMEM((examples, half, half), jnp.float32),
+            pltpu.SMEM((examples,), jnp.int32),
+            pltpu.SemaphoreType.DMA,
         ],
         compiler_params=pltpu.CompilerParams(
-            dimension_semantics=("arbitrary",), vmem_limit_bytes=28 << 20
+            dimension_semantics=("arbitrary",), vmem_limit_bytes=30 << 20
         ),
         name="example_norms",
-    )(lengths, in_hbm(acts), in_hbm(grads))
+    )(in_hbm(lengths), in_hbm(acts), in_hbm(grads))
 
 
 def on_chip(acts, order):

time: 104 us -> 103 us (level)
  transfers between devices with their start and end apart: 19 -> 19, of which waited for: 9 -> 9; matrix products, arithmetic and copies ran while one was open for 0% -> 0% of each run, Pallas kernels for 19% -> 20%
where the time goes in v2:
time: 103 us
  starting transfers between devices  34.7 us (34%)
  Pallas kernels  33 us (32%)
  waiting for transfers between devices  31.8 us (31%)
  local copies, waits for them, and re-layouts  2.05 us (2%)
    ppermute x16, starting transfers between devices, shift(): lax.ppermute(block, axis, [(i, (i + step) % count) for i in range(count)])  31.2 us
    ppermute x16, waiting for transfers between devices, shift(): lax.ppermute(block, axis, [(i, (i + step) % count) for i in range(count)])  30.2 us
    pallas_call x5, Pallas kernels, pieces(): pl.pallas_call(kernel, in_specs=[WHOLE] * (2 + len(order)), out_specs=[WH...  14.7 us
    pallas_call x1, Pallas kernels, example_norms(): pl.pallas_call(norm_kernel, grid=(NORM_STEPS,), in_specs=[pl.BlockSpec(me...  9.3 us
    pallas_call x1, Pallas kernels, on_chip(): pl.pallas_call(kernel, in_specs=[pl.BlockSpec(memory_space=pltpu.HBM), WH...  3.54 us
    ppermute x3, starting transfers between devices, partner_sum(): lax.ppermute(own, 'section', [(i, i ^ 1 << level) for i in range(count)])  3.45 us
    pallas_call x14, Pallas kernels, call(): pl.pallas_call(kernel, in_specs=[WHOLE] * len(args), out_specs=[WHOLE] *...  3.19 us
  transfers between devices with their start and end apart: 19, of which 9 were waited for; matrix products, arithmetic and copies ran while one was open for 0% of the time, Pallas kernels for 20%

profile of v2, /device:TPU:8, one launch (start us, length us, event | category | flops | bytes accessed | tf_op | source)
XLA Modules:
  0.0 102.9 jit_solution(6446772409372839247)
XLA Ops:
  0.6 0.0 copy-start
  0.6 0.0 copy-start.3
  0.6 9.3 %example_norms.1.own_ref = f32[2,8,128]{2,1,0:T(8,128)S(1)} custom-call(s32[2]{0:T(128)} %len_ref.1, bf16[2,512,4096]{2,1,0:T(8,128)(2,1)} %bitcast.8, bf16[2,512,1024]{2,1,0:T(8,128)(2,1)} %bitcast.6), custom_call_target="tpu_custom_call" | custom-call | tf_op jit(solution)/shard_map/example_norms/pallas_call | solution.py:112
  10.0 0.1 collective-permute-start.33
  10.1 1.2 %collective-permute-done.33.moved_ref = f32[2,8,128]{2,1,0:T(8,128)S(1)} collective-permute-done((f32[2,8,128]{2,1,0:T(8,128)S(1)}, f32[2,8,128]{2,1,0:T(8,128)S(1)}, u32[]{:S(2)}, u32[]{:S(2)}) %collective-permute-start.33) | collective-permute-done | bytes 8224 | tf_op jit(solution)/shard_map/ppermute | solution.py:38
  11.2 2.2 %collective-permute-start.34 = (f32[2,8,128]{2,1,0:T(8,128)S(1)}, f32[2,8,128]{2,1,0:T(8,128)S(1)}, u32[]{:S(2)}, u32[]{:S(2)}) collective-permute-start(f32[2,8,128]{2,1,0:T(8,128)S(1)} %shard_map.50.order_ref.own_ref), channel_id=1, source_target_pairs={{0,2},{1,3},{2,0},{3,1},{4,6},{5,7},{6,4},{7,5},{8,10},{9,11},{10,... | collective-permute-start | bytes 24584 | tf_op jit(solution)/shard_map/ppermute | solution.py:38
  13.4 1.2 %masked_rows.1 = (bf16[1024,1024]{1,0:T(8,128)(2,1)S(1)}, f32[8,128]{1,0:T(8,128)S(1)}) custom-call(s32[2]{0:T(128)S(1)} %copy-done.3, bf16[2,512,1024]{2,1,0:T(8,128)(2,1)S(1)} %bitcast.7, f32[2,8,128]{2,1,0:T(8,128)S(1)} %shard_map.50.order_ref.own_ref), custom_call_target="tpu_custom_call" | custom-call | tf_op jit(solution)/shard_map/masked_rows/pallas_call | solution.py:170
  14.7 1.3 %copy-done.1 = bf16[1024,1024]{1,0:T(8,128)(2,1)} copy-done((bf16[1024,1024]{1,0:T(8,128)(2,1)}, bf16[1024,1024]{1,0:T(8,128)(2,1)S(1)}, u32[]{:S(2)}) %copy-start.1) | copy-done | bytes 2097176
  16.0 0.0 collective-permute-done.34.moved_ref
  16.0 1.2 %collective-permute-start.35 = (f32[2,8,128]{2,1,0:T(8,128)S(1)}, f32[2,8,128]{2,1,0:T(8,128)S(1)}, u32[]{:S(2)}, u32[]{:S(2)}) collective-permute-start(f32[2,8,128]{2,1,0:T(8,128)S(1)} %shard_map.51.order_ref.own_ref), channel_id=1, source_target_pairs={{0,4},{1,5},{2,6},{3,7},{4,0},{5,1},{6,2},{7,3},{8,12},{9,13},{10,... | collective-permute-start | bytes 24584 | tf_op jit(solution)/shard_map/ppermute | solution.py:38
  17.2 3.5 %on_chip.1 = (bf16[2,512,4096]{2,1,0:T(8,128)(2,1)S(1)}, f32[8,128]{1,0:T(8,128)S(1)}) custom-call(bf16[2,512,4096]{2,1,0:T(8,128)(2,1)} %bitcast.9, f32[2,8,128]{2,1,0:T(8,128)S(1)} %shard_map.51.order_ref.own_ref), custom_call_target="tpu_custom_call" | custom-call | tf_op jit(solution)/shard_map/on_chip/pallas_call | solution.py:142
  20.7 0.4 collective-permute-done.35.moved_ref
  21.1 0.0 copy-done.2
  21.2 1.0 %clipped_rows.1 = (bf16[1024,1024]{1,0:T(8,128)(2,1)S(1)}, f32[2]{0:T(128)}) custom-call(f32[2,8,128]{2,1,0:T(8,128)S(1)} %shard_map.52.total_ref, bf16[1024,1024]{1,0:T(8,128)(2,1)S(1)} %copy-done.2), custom_call_target="tpu_custom_call" | custom-call | tf_op jit(solution)/shard_map/clipped_rows/pallas_call | solution.py:201
  22.2 80.0 %conditional.1 = (bf16[1,128,1024]{2,1,0:T(8,128)(2,1)S(1)}) conditional(s32[]{:T(128)} %convert_element_type.3, (bf16[2,512,4096]{2,1,0:T(8,128)(2,1)S(1)}, bf16[1024,1024]{1,0:T(8,128)(2,1)S(1)}) %tuple.16, (bf16[2,512,4096]{2,1,0:T(8,128)(2,1)S(1)}, bf16[1024,1024]{1,0:T(8,128)(2,1)S(1)}) %tuple.16), branch_computations={%region_0.1_spmd, %region_1.2_spmd} | conditional | bytes 32506544 | solution.py:450
  22.4 2.1 %terms.19 = (bf16[2,1024,128]{2,1,0:T(8,128)(2,1)S(1)}, bf16[2,1024,128]{2,1,0:T(8,128)(2,1)S(1)}, f32[8,128]{1,0:T(8,128)S(1)}) custom-call(bf16[2,512,4096]{2,1,0:T(8,128)(2,1)S(1)} %get-tuple-element.57.acts_ref, bf16[1024,1024]{1,0:T(8,128)(2,1)S(1)} %get-tuple-element.58.flip_ref), custom_call_target="tpu_custom_call" | custom-call | tf_op jit(solution)/shard_map/cond/branch_1_fun/terms/pallas_call | solution.py:242
  24.6 2.8 %collective-permute-start.18 = (bf16[2,1024,128]{2,1,0:T(8,128)(2,1)S(1)}, bf16[2,1024,128]{2,1,0:T(8,128)(2,1)S(1)}, u32[]{:S(2)}, u32[]{:S(2)}) collective-permute-start(bf16[2,1024,128]{2,1,0:T(8,128)(2,1)S(1)} %get-tuple-element.66), channel_id=1, source_target_pairs={{0,192},{64,0},{128,64},{192,128},{1,193},{65,1},{129,65},{193,129... | collective-permute-start | bytes 1572872 | tf_op jit(solution)/shard_map/cond/branch_1_fun/ppermute | solution.py:56
  27.4 3.4 %terms.20 = (bf16[4,1024,128]{2,1,0:T(8,128)(2,1)S(1)}, bf16[4,1024,128]{2,1,0:T(8,128)(2,1)S(1)}, f32[8,128]{1,0:T(8,128)S(1)}) custom-call(bf16[2,512,4096]{2,1,0:T(8,128)(2,1)S(1)} %get-tuple-element.57.acts_ref, bf16[1024,1024]{1,0:T(8,128)(2,1)S(1)} %get-tuple-element.58.flip_ref, f32[8,128]{1,0:T(8,128)S(1)} %get-tuple-element.59.refs_0_), custom_call_target="tpu_custom_call" | custom-call | tf_op jit(solution)/shard_map/cond/branch_1_fun/terms/pallas_call | solution.py:242
  30.8 0.1 collective-permute-start.19
  30.9 0.8 collective-permute-start.17
  31.6 2.6 %collective-permute-start.23 = (bf16[4,1024,128]{2,1,0:T(8,128)(2,1)S(1)}, bf16[4,1024,128]{2,1,0:T(8,128)(2,1)S(1)}, u32[]{:S(2)}, u32[]{:S(2)}) collective-permute-start(bf16[4,1024,128]{2,1,0:T(8,128)(2,1)S(1)} %get-tuple-element.76), channel_id=1, source_target_pairs={{0,192},{64,0},{128,64},{192,128},{1,193},{65,1},{129,65},{193,129... | collective-permute-start | bytes 3145736 | tf_op jit(solution)/shard_map/cond/branch_1_fun/ppermute | solution.py:56
  34.2 3.4 %terms.21 = (bf16[2,1024,128]{2,1,0:T(8,128)(2,1)S(1)}, bf16[2,1024,128]{2,1,0:T(8,128)(2,1)S(1)}, bf16[4,1024,128]{2,1,0:T(8,128)(2,1)S(1)}, f32[8,128]{1,0:T(8,128)S(1)}) custom-call(bf16[2,512,4096]{2,1,0:T(8,128)(2,1)S(1)} %get-tuple-element.57.acts_ref, bf16[1024,1024]{1,0:T(8,128)(2,1)S(1)} %get-tuple-element.58.flip_ref, ...), custom_call_target="tpu_custom_call" | custom-call | tf_op jit(solution)/shard_map/cond/branch_1_fun/terms/pallas_call | solution.py:242
  37.5 0.0 collective-permute-done.18.got_ref
  37.6 0.1 branch_1_fun.12
  37.7 2.0 %collective-permute-start.26 = (bf16[2,1024,128]{2,1,0:T(8,128)(2,1)S(1)}, bf16[2,1024,128]{2,1,0:T(8,128)(2,1)S(1)}, u32[]{:S(2)}, u32[]{:S(2)}) collective-permute-start(bf16[2,1024,128]{2,1,0:T(8,128)(2,1)S(1)} %get-tuple-element.82), channel_id=1, source_target_pairs={{0,192},{64,0},{128,64},{192,128},{1,193},{65,1},{129,65},{193,129... | collective-permute-start | bytes 1572872 | tf_op jit(solution)/shard_map/cond/branch_1_fun/ppermute | solution.py:56
  39.7 12.7 %collective-permute-done.17.got_ref = bf16[2,1024,128]{2,1,0:T(8,128)(2,1)S(1)} collective-permute-done((bf16[2,1024,128]{2,1,0:T(8,128)(2,1)S(1)}, bf16[2,1024,128]{2,1,0:T(8,128)(2,1)S(1)}, u32[]{:S(2)}, u32[]{:S(2)}) %collective-permute-start.17) | collective-permute-done | bytes 524320 | tf_op jit(solution)/shard_map/cond/branch_1_fun/ppermute | solution.py:56
  52.5 0.1 branch_1_fun.11
  52.6 0.1 collective-permute-start.25
  52.7 2.1 %terms.22 = (bf16[2,1024,128]{2,1,0:T(8,128)(2,1)S(1)}, bf16[2,1024,128]{2,1,0:T(8,128)(2,1)S(1)}, f32[8,128]{1,0:T(8,128)S(1)}) custom-call(bf16[2,512,4096]{2,1,0:T(8,128)(2,1)S(1)} %get-tuple-element.57.acts_ref, bf16[1024,1024]{1,0:T(8,128)(2,1)S(1)} %get-tuple-element.58.flip_ref, f32[8,128]{1,0:T(8,128)S(1)} %get-tuple-element.61.refs_0_, ...), custom_call_target="tpu_custom_call" | custom-call | tf_op jit(solution)/shard_map/cond/branch_1_fun/terms/pallas_call | solution.py:242
  54.8 3.3 %collective-permute-start.21 = (bf16[2,1024,128]{2,1,0:T(8,128)(2,1)S(1)}, bf16[2,1024,128]{2,1,0:T(8,128)(2,1)S(1)}, u32[]{:S(2)}, u32[]{:S(2)}) collective-permute-start(bf16[2,1024,128]{2,1,0:T(8,128)(2,1)S(1)} %get-tuple-element.73), channel_id=1, source_target_pairs={{0,192},{64,0},{128,64},{192,128},{1,193},{65,1},{129,65},{193,129... | collective-permute-start | bytes 1572872 | tf_op jit(solution)/shard_map/cond/branch_1_fun/ppermute | solution.py:56
  58.1 3.7 %terms.23 = (bf16[2,1024,128]{2,1,0:T(8,128)(2,1)S(1)}, bf16[2,1024,128]{2,1,0:T(8,128)(2,1)S(1)}, bf16[4,1024,128]{2,1,0:T(8,128)(2,1)S(1)}, f32[8,128]{1,0:T(8,128)}) custom-call(bf16[2,512,4096]{2,1,0:T(8,128)(2,1)S(1)} %get-tuple-element.57.acts_ref, bf16[1024,1024]{1,0:T(8,128)(2,1)S(1)} %get-tuple-element.58.flip_ref, ...), custom_call_target="tpu_custom_call" | custom-call | tf_op jit(solution)/shard_map/cond/branch_1_fun/terms/pallas_call | solution.py:242
  61.9 0.0 collective-permute-done.19.got_ref.refs_3_
  61.9 0.0 collective-permute-start.22
  61.9 0.0 collective-permute-done.23.got_ref.refs_2_
  61.9 0.0 collective-permute-done.26.refs_4_
  61.9 1.2 %collective-permute-done.25.refs_1_ = bf16[2,1024,128]{2,1,0:T(8,128)(2,1)S(1)} collective-permute-done((bf16[2,1024,128]{2,1,0:T(8,128)(2,1)S(1)}, bf16[2,1024,128]{2,1,0:T(8,128)(2,1)S(1)}, u32[]{:S(2)}, u32[]{:S(2)}) %collective-permute-start.25) | collective-permute-done | bytes 524320 | tf_op jit(solution)/shard_map/cond/branch_1_fun/ppermute | solution.py:56
  63.1 0.4 branch_1_fun.16
  63.5 5.9 %collective-permute-start.29 = (bf16[1024,128]{1,0:T(8,128)(2,1)S(1)}, bf16[1024,128]{1,0:T(8,128)(2,1)S(1)}, u32[]{:S(2)}, u32[]{:S(2)}) collective-permute-start(bf16[1024,128]{1,0:T(8,128)(2,1)S(1)} %get-tuple-element.87), channel_id=1, source_target_pairs={{0,56},{8,0},{16,8},{24,16},{32,24},{40,32},{48,40},{56,48},{1,57}... | collective-permute-start | bytes 786440 | tf_op jit(solution)/shard_map/cond/branch_1_fun/ppermute | solution.py:56
  69.4 0.7 branch_1_fun.13
  70.1 0.0 collective-permute-start.20
  70.1 0.7 branch_1_fun.14
  70.8 3.2 %collective-permute-start.24 = (bf16[2,1024,128]{2,1,0:T(8,128)(2,1)S(1)}, bf16[2,1024,128]{2,1,0:T(8,128)(2,1)S(1)}, u32[]{:S(2)}, u32[]{:S(2)}) collective-permute-start(bf16[2,1024,128]{2,1,0:T(8,128)(2,1)S(1)} %get-tuple-element.77), channel_id=1, source_target_pairs={{0,192},{64,0},{128,64},{192,128},{1,193},{65,1},{129,65},{193,129... | collective-permute-start | bytes 1572872 | tf_op jit(solution)/shard_map/cond/branch_1_fun/ppermute | solution.py:56
  74.0 0.0 collective-permute-done.29.got_ref
  74.0 0.0 collective-permute-start.27
  74.0 0.1 branch_1_fun.18
  74.1 0.0 collective-permute-done.21.refs_2_
  74.1 3.3 %collective-permute-start.30 = (bf16[1024,128]{1,0:T(8,128)(2,1)S(1)}, bf16[1024,128]{1,0:T(8,128)(2,1)S(1)}, u32[]{:S(2)}, u32[]{:S(2)}) collective-permute-start(bf16[1024,128]{1,0:T(8,128)(2,1)S(1)} %branch_1_fun.18), channel_id=1, source_target_pairs={{0,56},{8,0},{16,8},{24,16},{32,24},{40,32},{48,40},{56,48},{1,57}... | collective-permute-start | bytes 786440 | tf_op jit(solution)/shard_map/cond/branch_1_fun/ppermute | solution.py:56
  77.4 0.0 collective-permute-done.22.refs_3_
  77.4 7.3 %collective-permute-done.20.refs_1_ = bf16[2,1024,128]{2,1,0:T(8,128)(2,1)S(1)} collective-permute-done((bf16[2,1024,128]{2,1,0:T(8,128)(2,1)S(1)}, bf16[2,1024,128]{2,1,0:T(8,128)(2,1)S(1)}, u32[]{:S(2)}, u32[]{:S(2)}) %collective-permute-start.20) | collective-permute-done | bytes 524320 | tf_op jit(solution)/shard_map/cond/branch_1_fun/ppermute | solution.py:56
  84.7 1.3 %collective-permute-done.24.refs_4_ = bf16[2,1024,128]{2,1,0:T(8,128)(2,1)S(1)} collective-permute-done((bf16[2,1024,128]{2,1,0:T(8,128)(2,1)S(1)}, bf16[2,1024,128]{2,1,0:T(8,128)(2,1)S(1)}, u32[]{:S(2)}, u32[]{:S(2)}) %collective-permute-start.24) | collective-permute-done | bytes 524320 | tf_op jit(solution)/shard_map/cond/branch_1_fun/ppermute | solution.py:56
  86.0 0.4 branch_1_fun.15
  86.4 0.0 collective-permute-done.30.got_ref
  86.4 0.1 branch_1_fun.19
  86.5 3.3 %collective-permute-start.31 = (bf16[1024,128]{1,0:T(8,128)(2,1)S(1)}, bf16[1024,128]{1,0:T(8,128)(2,1)S(1)}, u32[]{:S(2)}, u32[]{:S(2)}) collective-permute-start(bf16[1024,128]{1,0:T(8,128)(2,1)S(1)} %branch_1_fun.19), channel_id=1, source_target_pairs={{0,56},{8,0},{16,8},{24,16},{32,24},{40,32},{48,40},{56,48},{1,57}... | collective-permute-start | bytes 786440 | tf_op jit(solution)/shard_map/cond/branch_1_fun/ppermute | solution.py:56
  89.9 0.0 collective-permute-done.27.got_ref.refs_3_
  89.9 0.1 branch_1_fun.17
  89.9 0.1 collective-permute-start.28
  90.0 3.7 %collective-permute-done.31.got_ref = bf16[1024,128]{1,0:T(8,128)(2,1)S(1)} collective-permute-done((bf16[1024,128]{1,0:T(8,128)(2,1)S(1)}, bf16[1024,128]{1,0:T(8,128)(2,1)S(1)}, u32[]{:S(2)}, u32[]{:S(2)}) %collective-permute-start.31) | collective-permute-done | bytes 262176 | tf_op jit(solution)/shard_map/cond/branch_1_fun/ppermute | solution.py:56
  93.7 0.1 branch_1_fun.20
  93.8 3.8 %collective-permute-start.32 = (bf16[1024,128]{1,0:T(8,128)(2,1)S(1)}, bf16[1024,128]{1,0:T(8,128)(2,1)S(1)}, u32[]{:S(2)}, u32[]{:S(2)}) collective-permute-start(bf16[1024,128]{1,0:T(8,128)(2,1)S(1)} %branch_1_fun.20), channel_id=1, source_target_pairs={{0,56},{8,0},{16,8},{24,16},{32,24},{40,32},{48,40},{56,48},{1,57}... | collective-permute-start | bytes 786440 | tf_op jit(solution)/shard_map/cond/branch_1_fun/ppermute | solution.py:56
  97.6 3.1 %collective-permute-done.28.refs_1_ = bf16[1024,128]{1,0:T(8,128)(2,1)S(1)} collective-permute-done((bf16[1024,128]{1,0:T(8,128)(2,1)S(1)}, bf16[1024,128]{1,0:T(8,128)(2,1)S(1)}, u32[]{:S(2)}, u32[]{:S(2)}) %collective-permute-start.28) | collective-permute-done | bytes 262176 | tf_op jit(solution)/shard_map/cond/branch_1_fun/ppermute | solution.py:56
  100.8 0.7 collective-permute-done.32.refs_2_
  101.5 0.4 branch_1_fun.21
  102.2 0.7 copy.7
  (7 shorter events, 0.0 us)
Async XLA Ops:
  0.6 12.8 %copy-start = (bf16[1,2,512,1024]{3,2,1,0:T(8,128)(2,1)S(1)}, bf16[1,2,512,1024]{3,2,1,0:T(8,128)(2,1)}, u32[]{:S(2)}) copy-start(bf16[1,2,512,1024]{3,2,1,0:T(8,128)(2,1)} %param.6) | copy-start | bytes 6291460
  0.6 12.7 %copy-start.3 = (s32[2]{0:T(128)S(1)}, s32[2]{0:T(128)}, u32[]{:S(2)}) copy-start(s32[2]{0:T(128)} %len_ref.1) | copy-start | bytes 28
  10.0 1.3 %collective-permute-start.33 = (f32[2,8,128]{2,1,0:T(8,128)S(1)}, f32[2,8,128]{2,1,0:T(8,128)S(1)}, u32[]{:S(2)}, u32[]{:S(2)}) collective-permute-start(f32[2,8,128]{2,1,0:T(8,128)S(1)} %example_norms.1.own_ref), channel_id=1, source_target_pairs={{0,1},{1,0},{2,3},{3,2},{4,5},{5,4},{6,7},{7,6},{8,9},{9,8},{10,11... | collective-permute-start | bytes 24584 | tf_op jit(solution)/shard_map/ppermute | solution.py:38
  11.2 4.7 %collective-permute-start.34 = (f32[2,8,128]{2,1,0:T(8,128)S(1)}, f32[2,8,128]{2,1,0:T(8,128)S(1)}, u32[]{:S(2)}, u32[]{:S(2)}) collective-permute-start(f32[2,8,128]{2,1,0:T(8,128)S(1)} %shard_map.50.order_ref.own_ref), channel_id=1, source_target_pairs={{0,2},{1,3},{2,0},{3,1},{4,6},{5,7},{6,4},{7,5},{8,10},{9,11},{10,... | collective-permute-start | bytes 24584 | tf_op jit(solution)/shard_map/ppermute | solution.py:38
  14.6 1.3 %copy-start.1 = (bf16[1024,1024]{1,0:T(8,128)(2,1)}, bf16[1024,1024]{1,0:T(8,128)(2,1)S(1)}, u32[]{:S(2)}) copy-start(bf16[1024,1024]{1,0:T(8,128)(2,1)S(1)} %get-tuple-element.99.flip_ref) | copy-start | bytes 6291460
  16.0 5.2 %collective-permute-start.35 = (f32[2,8,128]{2,1,0:T(8,128)S(1)}, f32[2,8,128]{2,1,0:T(8,128)S(1)}, u32[]{:S(2)}, u32[]{:S(2)}) collective-permute-start(f32[2,8,128]{2,1,0:T(8,128)S(1)} %shard_map.51.order_ref.own_ref), channel_id=1, source_target_pairs={{0,4},{1,5},{2,6},{3,7},{4,0},{5,1},{6,2},{7,3},{8,12},{9,13},{10,... | collective-permute-start | bytes 24584 | tf_op jit(solution)/shard_map/ppermute | solution.py:38
  17.2 4.0 %copy-start.2 = (bf16[1024,1024]{1,0:T(8,128)(2,1)S(1)}, bf16[1024,1024]{1,0:T(8,128)(2,1)}, u32[]{:S(2)}) copy-start(bf16[1024,1024]{1,0:T(8,128)(2,1)} %copy-done.1) | copy-start | bytes 6291460
  24.6 13.0 %collective-permute-start.18 = (bf16[2,1024,128]{2,1,0:T(8,128)(2,1)S(1)}, bf16[2,1024,128]{2,1,0:T(8,128)(2,1)S(1)}, u32[]{:S(2)}, u32[]{:S(2)}) collective-permute-start(bf16[2,1024,128]{2,1,0:T(8,128)(2,1)S(1)} %get-tuple-element.66), channel_id=1, source_target_pairs={{0,192},{64,0},{128,64},{192,128},{1,193},{65,1},{129,65},{193,129... | collective-permute-start | bytes 1572872 | tf_op jit(solution)/shard_map/cond/branch_1_fun/ppermute | solution.py:56
  30.8 31.1 %collective-permute-start.19 = (bf16[4,1024,128]{2,1,0:T(8,128)(2,1)S(1)}, bf16[4,1024,128]{2,1,0:T(8,128)(2,1)S(1)}, u32[]{:S(2)}, u32[]{:S(2)}) collective-permute-start(bf16[4,1024,128]{2,1,0:T(8,128)(2,1)S(1)} %get-tuple-element.71), channel_id=1, source_target_pairs={{0,64},{64,128},{128,192},{192,0},{1,65},{65,129},{129,193},{193,1... | collective-permute-start | bytes 3145736 | tf_op jit(solution)/shard_map/cond/branch_1_fun/ppermute | solution.py:56
  30.9 21.6 %collective-permute-start.17 = (bf16[2,1024,128]{2,1,0:T(8,128)(2,1)S(1)}, bf16[2,1024,128]{2,1,0:T(8,128)(2,1)S(1)}, u32[]{:S(2)}, u32[]{:S(2)}) collective-permute-start(bf16[2,1024,128]{2,1,0:T(8,128)(2,1)S(1)} %get-tuple-element.63), channel_id=1, source_target_pairs={{0,64},{64,128},{128,192},{192,0},{1,65},{65,129},{129,193},{193,1... | collective-permute-start | bytes 1572872 | tf_op jit(solution)/shard_map/cond/branch_1_fun/ppermute | solution.py:56
  31.6 30.2 %collective-permute-start.23 = (bf16[4,1024,128]{2,1,0:T(8,128)(2,1)S(1)}, bf16[4,1024,128]{2,1,0:T(8,128)(2,1)S(1)}, u32[]{:S(2)}, u32[]{:S(2)}) collective-permute-start(bf16[4,1024,128]{2,1,0:T(8,128)(2,1)S(1)} %get-tuple-element.76), channel_id=1, source_target_pairs={{0,192},{64,0},{128,64},{192,128},{1,193},{65,1},{129,65},{193,129... | collective-permute-start | bytes 3145736 | tf_op jit(solution)/shard_map/cond/branch_1_fun/ppermute | solution.py:56
  37.7 24.2 %collective-permute-start.26 = (bf16[2,1024,128]{2,1,0:T(8,128)(2,1)S(1)}, bf16[2,1024,128]{2,1,0:T(8,128)(2,1)S(1)}, u32[]{:S(2)}, u32[]{:S(2)}) collective-permute-start(bf16[2,1024,128]{2,1,0:T(8,128)(2,1)S(1)} %get-tuple-element.82), channel_id=1, source_target_pairs={{0,192},{64,0},{128,64},{192,128},{1,193},{65,1},{129,65},{193,129... | collective-permute-start | bytes 1572872 | tf_op jit(solution)/shard_map/cond/branch_1_fun/ppermute | solution.py:56
  52.6 10.5 %collective-permute-start.25 = (bf16[2,1024,128]{2,1,0:T(8,128)(2,1)S(1)}, bf16[2,1024,128]{2,1,0:T(8,128)(2,1)S(1)}, u32[]{:S(2)}, u32[]{:S(2)}) collective-permute-start(bf16[2,1024,128]{2,1,0:T(8,128)(2,1)S(1)} %get-tuple-element.81), channel_id=1, source_target_pairs={{0,64},{64,128},{128,192},{192,0},{1,65},{65,129},{129,193},{193,1... | collective-permute-start | bytes 1572872 | tf_op jit(solution)/shard_map/cond/branch_1_fun/ppermute | solution.py:56
  54.8 19.2 %collective-permute-start.21 = (bf16[2,1024,128]{2,1,0:T(8,128)(2,1)S(1)}, bf16[2,1024,128]{2,1,0:T(8,128)(2,1)S(1)}, u32[]{:S(2)}, u32[]{:S(2)}) collective-permute-start(bf16[2,1024,128]{2,1,0:T(8,128)(2,1)S(1)} %get-tuple-element.73), channel_id=1, source_target_pairs={{0,192},{64,0},{128,64},{192,128},{1,193},{65,1},{129,65},{193,129... | collective-permute-start | bytes 1572872 | tf_op jit(solution)/shard_map/cond/branch_1_fun/ppermute | solution.py:56
  61.9 15.6 %collective-permute-start.22 = (bf16[2,1024,128]{2,1,0:T(8,128)(2,1)S(1)}, bf16[2,1024,128]{2,1,0:T(8,128)(2,1)S(1)}, u32[]{:S(2)}, u32[]{:S(2)}) collective-permute-start(bf16[2,1024,128]{2,1,0:T(8,128)(2,1)S(1)} %get-tuple-element.74), channel_id=1, source_target_pairs={{0,64},{64,128},{128,192},{192,0},{1,65},{65,129},{129,193},{193,1... | collective-permute-start | bytes 1572872 | tf_op jit(solution)/shard_map/cond/branch_1_fun/ppermute | solution.py:56
  63.5 10.5 %collective-permute-start.29 = (bf16[1024,128]{1,0:T(8,128)(2,1)S(1)}, bf16[1024,128]{1,0:T(8,128)(2,1)S(1)}, u32[]{:S(2)}, u32[]{:S(2)}) collective-permute-start(bf16[1024,128]{1,0:T(8,128)(2,1)S(1)} %get-tuple-element.87), channel_id=1, source_target_pairs={{0,56},{8,0},{16,8},{24,16},{32,24},{40,32},{48,40},{56,48},{1,57}... | collective-permute-start | bytes 786440 | tf_op jit(solution)/shard_map/cond/branch_1_fun/ppermute | solution.py:56
  70.1 14.6 %collective-permute-start.20 = (bf16[2,1024,128]{2,1,0:T(8,128)(2,1)S(1)}, bf16[2,1024,128]{2,1,0:T(8,128)(2,1)S(1)}, u32[]{:S(2)}, u32[]{:S(2)}) collective-permute-start(bf16[2,1024,128]{2,1,0:T(8,128)(2,1)S(1)} %get-tuple-element.72), channel_id=1, source_target_pairs={{0,64},{64,128},{128,192},{192,0},{1,65},{65,129},{129,193},{193,1... | collective-permute-start | bytes 1572872 | tf_op jit(solution)/shard_map/cond/branch_1_fun/ppermute | solution.py:56
  70.8 15.3 %collective-permute-start.24 = (bf16[2,1024,128]{2,1,0:T(8,128)(2,1)S(1)}, bf16[2,1024,128]{2,1,0:T(8,128)(2,1)S(1)}, u32[]{:S(2)}, u32[]{:S(2)}) collective-permute-start(bf16[2,1024,128]{2,1,0:T(8,128)(2,1)S(1)} %get-tuple-element.77), channel_id=1, source_target_pairs={{0,192},{64,0},{128,64},{192,128},{1,193},{65,1},{129,65},{193,129... | collective-permute-start | bytes 1572872 | tf_op jit(solution)/shard_map/cond/branch_1_fun/ppermute | solution.py:56
  74.0 15.9 %collective-permute-start.27 = (bf16[2,1024,128]{2,1,0:T(8,128)(2,1)S(1)}, bf16[2,1024,128]{2,1,0:T(8,128)(2,1)S(1)}, u32[]{:S(2)}, u32[]{:S(2)}) collective-permute-start(bf16[2,1024,128]{2,1,0:T(8,128)(2,1)S(1)} %get-tuple-element.83), channel_id=1, source_target_pairs={{0,8},{8,16},{16,24},{24,32},{32,40},{40,48},{48,56},{56,0},{1,9},... | collective-permute-start | bytes 1572872 | tf_op jit(solution)/shard_map/cond/branch_1_fun/ppermute | solution.py:56
  74.1 12.3 %collective-permute-start.30 = (bf16[1024,128]{1,0:T(8,128)(2,1)S(1)}, bf16[1024,128]{1,0:T(8,128)(2,1)S(1)}, u32[]{:S(2)}, u32[]{:S(2)}) collective-permute-start(bf16[1024,128]{1,0:T(8,128)(2,1)S(1)} %branch_1_fun.18), channel_id=1, source_target_pairs={{0,56},{8,0},{16,8},{24,16},{32,24},{40,32},{48,40},{56,48},{1,57}... | collective-permute-start | bytes 786440 | tf_op jit(solution)/shard_map/cond/branch_1_fun/ppermute | solution.py:56
  86.5 7.2 %collective-permute-start.31 = (bf16[1024,128]{1,0:T(8,128)(2,1)S(1)}, bf16[1024,128]{1,0:T(8,128)(2,1)S(1)}, u32[]{:S(2)}, u32[]{:S(2)}) collective-permute-start(bf16[1024,128]{1,0:T(8,128)(2,1)S(1)} %branch_1_fun.19), channel_id=1, source_target_pairs={{0,56},{8,0},{16,8},{24,16},{32,24},{40,32},{48,40},{56,48},{1,57}... | collective-permute-start | bytes 786440 | tf_op jit(solution)/shard_map/cond/branch_1_fun/ppermute | solution.py:56
  89.9 10.8 %collective-permute-start.28 = (bf16[1024,128]{1,0:T(8,128)(2,1)S(1)}, bf16[1024,128]{1,0:T(8,128)(2,1)S(1)}, u32[]{:S(2)}, u32[]{:S(2)}) collective-permute-start(bf16[1024,128]{1,0:T(8,128)(2,1)S(1)} %branch_1_fun.17), channel_id=1, source_target_pairs={{0,16},{8,24},{16,32},{24,40},{32,48},{40,56},{48,0},{56,8},{1,17}... | collective-permute-start | bytes 786440 | tf_op jit(solution)/shard_map/cond/branch_1_fun/ppermute | solution.py:56
  93.8 7.7 %collective-permute-start.32 = (bf16[1024,128]{1,0:T(8,128)(2,1)S(1)}, bf16[1024,128]{1,0:T(8,128)(2,1)S(1)}, u32[]{:S(2)}, u32[]{:S(2)}) collective-permute-start(bf16[1024,128]{1,0:T(8,128)(2,1)S(1)} %branch_1_fun.20), channel_id=1, source_target_pairs={{0,56},{8,0},{16,8},{24,16},{32,24},{40,32},{48,40},{56,48},{1,57}... | collective-permute-start | bytes 786440 | tf_op jit(solution)/shard_map/cond/branch_1_fun/ppermute | solution.py:56
